TPU v7x, 512 devices: a whole 4x8x8 slice. The times are simulated.
512 devices in a mesh: row: 32 (over y, x), col: 16 (over z, core).
Axes of the slice: x: 4, y: 8, z: 8, core: 2. Of those that a mesh axis runs over, the one named last changes fastest.
Arguments:
- tokens: bfloat16 [24576, 2048], P('row', 'col'), may hold values from -6 to 6
- out_grad: bfloat16 [24576, 2048], P('row', 'col'), may hold values from -3072 to 3072
- counts: int32 [32], P('row'), may hold values from 65 to 768
- block_moves: int32 [16, 3], replicated, may hold values from 0 to 31, as said below
- segment_ids: int32 [24576], P('row'), may hold values from 0 to 767, never falling along the last dimension, each value on 1 to 128 neighbouring positions
- gate_weight: bfloat16 [2048, 8192], P('row', 'col'), may hold values from -0.125 to 0.125
- up_weight: bfloat16 [2048, 8192], P('row', 'col'), may hold values from -0.125 to 0.125
- down_weight: bfloat16 [2048, 8192], P('row', 'col'), may hold values from -0.0625 to 0.0625
Outputs:
- hidden: bfloat16 [16384, 8192], P('row', 'col')
- gate_grad: float32 [2048, 8192], P('row', 'col')
- up_grad: float32 [2048, 8192], P('row', 'col')
- down_grad: float32 [2048, 8192], P('row', 'col')
Inputs may be any that keep to these rules, and one draw needn't show every extreme that they name: `block_moves`: each row is (source rank, destination rank, block index); the block is a valid block of its source; no two rows share both source and destination, nor both source and block; a rank is the source of at most two rows or the destination of at most one, never both; after the moves every rank holds at most 4 valid blocks and some hold exactly 4. `segment_ids`: never falling along the whole array; each document covers 1 to 128 consecutive slots.
All inputs are finite; a program needn't handle non-finite values.
Results may differ from a plain program's by a relative error of at most 0.015.
Values may be sent and summed in bfloat16 or wider, within the bound.
No kernel may reach another device: no remote copies, remote signals or barrier semaphores. Data moves between devices by JAX's collectives and lax.ppermute only.
A program may use at most 64 MiB of HBM per device.

v0:
```python
import jax
import jax.numpy as jnp
from jax import lax
from jax.experimental import pallas as pl
from jax.experimental.pallas import tpu as pltpu
from jax.sharding import Mesh
from jax.sharding import PartitionSpec as P


BLOCK = 128
WORK = 4
CAP = 6
NY, NX, NZ = 8, 4, 8
ROW = ("y", "x")
COL = ("z", "c")
NTAG = 16
CUT = 128


def vmem():
    return pl.BlockSpec(memory_space=pltpu.VMEM)


def smem():
    return pl.BlockSpec(memory_space=pltpu.SMEM)


def params(mib, **kw):
    return pltpu.CompilerParams(vmem_limit_bytes=mib * 1024 * 1024, **kw)


def move_count(moves):
    return moves.shape[1]


def pack_x(pos, moves, seg, tok, grad, box, work, masked):
    me = pos[0] * NX + pos[1]
    count = pos[2]
    span = WORK * BLOCK
    ids = seg[...]
    lane = lax.broadcasted_iota(jnp.int32, (CAP, BLOCK), 1)
    row = lax.broadcasted_iota(jnp.int32, (CAP, BLOCK), 0)
    ahead = jnp.concatenate([ids[1:], ids[-1:]], axis=0)
    joined = jnp.concatenate([ids[:, 1:], ahead[:, :1]], axis=1)
    mask = ((row * BLOCK + lane + 1 < count) & (joined == ids)).astype(jnp.float32)
    for b in range(CAP):
        rows = slice(b * BLOCK, (b + 1) * BLOCK)
        wide = jnp.broadcast_to(mask[b : b + 1, :], (BLOCK, BLOCK)).T
        masked[rows, :] = (grad[rows, :].astype(jnp.float32) * wide).astype(jnp.bfloat16)
    tally = jnp.sum(mask, axis=0, keepdims=True)
    for d in range(NX):
        box[d, 4 * BLOCK :, :] = jnp.broadcast_to(tally, (NTAG, BLOCK)).astype(jnp.bfloat16)

    def body(m, seen):
        src, dst, blk = moves[0, m], moves[1, m], moves[2, m]
        mine = src == me

        @pl.when(mine)
        def _():
            peer = dst % NX
            at = pl.multiple_of(seen * (2 * BLOCK), BLOCK)
            start = pl.multiple_of(blk * BLOCK, BLOCK)
            box[peer, pl.ds(at, BLOCK), :] = tok[pl.ds(start, BLOCK), :]
            box[peer, pl.ds(at + BLOCK, BLOCK), :] = masked[pl.ds(start, BLOCK), :]

        return jnp.where(mine, jnp.minimum(seen + 1, 1), seen)

    lax.fori_loop(0, move_count(moves), body, 0)
    work[...] = jnp.zeros_like(work)

    def own(b, nth):
        def gone(m, hit):
            return hit | ((moves[0, m] == me) & (moves[2, m] == b)).astype(jnp.int32)

        left = lax.fori_loop(0, move_count(moves), gone, 0)
        keep = (b * BLOCK < count) & (left == 0)

        @pl.when(keep & (nth < WORK))
        def _():
            start = pl.multiple_of(b * BLOCK, BLOCK)
            at = pl.multiple_of(nth * BLOCK, BLOCK)
            work[pl.ds(at, BLOCK), :] = tok[pl.ds(start, BLOCK), :]
            work[pl.ds(at + span, BLOCK), :] = masked[pl.ds(start, BLOCK), :]

        return nth + keep.astype(jnp.int32)

    lax.fori_loop(0, CAP, own, 0)


def pack_y(pos, moves, got, box, seen):
    my, mx = pos[0], pos[1]
    for i in range(NX):
        seen[i] = 0
    tally = got[0, 4 * BLOCK :, :].astype(jnp.float32)
    for i in range(1, NX):
        tally = tally + got[i, 4 * BLOCK :, :].astype(jnp.float32)
    for d in range(NY):
        box[d, 2 * BLOCK :, :] = tally.astype(jnp.bfloat16)

    def body(m, carry):
        src, dst = moves[0, m], moves[1, m]

        @pl.when(src // NX == my)
        def _():
            sx = src % NX
            nth = seen[sx]
            seen[sx] = jnp.minimum(nth + 1, 1)

            @pl.when(dst % NX == mx)
            def _():
                at = pl.multiple_of(nth * (2 * BLOCK), BLOCK)
                box[dst // NX, : 2 * BLOCK, :] = got[sx, pl.ds(at, 2 * BLOCK), :]

        return carry

    lax.fori_loop(0, move_count(moves), body, 0)


def pick_arrival(pos, moves, got, box, total):
    me = pos[0] * NX + pos[1]
    tally = got[0, 2 * BLOCK : 2 * BLOCK + 8, :].astype(jnp.float32)
    for i in range(1, NY):
        tally = tally + got[i, 2 * BLOCK : 2 * BLOCK + 8, :].astype(jnp.float32)
    total[...] = jnp.broadcast_to(jnp.sum(tally, axis=1, keepdims=True), total.shape)

    def came(m, at):
        return jnp.where(moves[1, m] == me, moves[0, m] // NX, at)

    sy = lax.fori_loop(0, move_count(moves), came, 0)
    for d in range(NZ):
        box[d] = got[sy, : 2 * BLOCK, :]


def gather_up(pos, *refs):
    pieces, late, out = refs[:NZ], refs[NZ], refs[NZ + 1]
    rows = pieces[0].shape[0]
    for k, piece in enumerate(pieces):
        out[k, :rows, :] = piece[...]
        out[k, rows:, :] = late[(pos[4] - k + NZ) % NZ]


def lay_out(pos, moves, mine, other, tok, grad):
    me = pos[0] * NX + pos[1]
    first = pos[3] == 0
    my_z = pos[4]
    span = WORK * BLOCK

    def own(b, nth):
        def gone(m, hit):
            return hit | ((moves[0, m] == me) & (moves[2, m] == b)).astype(jnp.int32)

        left = lax.fori_loop(0, move_count(moves), gone, 0)
        return nth + ((b * BLOCK < pos[2]) & (left == 0)).astype(jnp.int32)

    def came(m, hit):
        return hit | (moves[1, m] == me).astype(jnp.int32)

    nth = lax.fori_loop(0, CAP, own, 0)
    here = lax.fori_loop(0, move_count(moves), came, 0)

    def pick(z, side, low, size):
        away = (my_z - z + NZ) % NZ
        take = first if side == 0 else jnp.logical_not(first)
        rows = slice(low, low + size)
        return jnp.where(take, mine[away, rows, :], other[away, rows, :])

    for z in range(NZ):
        for side in range(2):
            cols = slice((2 * z + side) * BLOCK, (2 * z + side + 1) * BLOCK)
            tok[:, cols] = pick(z, side, 0, span)
            grad[:, cols] = pick(z, side, span, span)

    @pl.when((here == 1) & (nth < WORK))
    def _():
        rows = pl.ds(pl.multiple_of(nth * BLOCK, BLOCK), BLOCK)
        for z in range(NZ):
            for side in range(2):
                cols = slice((2 * z + side) * BLOCK, (2 * z + side + 1) * BLOCK)
                tok[rows, cols] = pick(z, side, 2 * span, BLOCK)
                grad[rows, cols] = pick(z, side, 2 * span + BLOCK, BLOCK)


def compute(
    total, tok_in, grad_in, weights, hidden, by_x, by_y,
    tok, grad, held, hid, back, stage, in_sem, out_sem, hid_sem,
):
    width = hid.shape[1]
    tile = width // 2
    per = by_x.shape[2]
    cut = by_x.shape[3] - width
    loads = (
        pltpu.make_async_copy(tok_in, tok, in_sem.at[0]),
        pltpu.make_async_copy(grad_in, grad, in_sem.at[1]),
        pltpu.make_async_copy(weights, held, in_sem.at[2]),
    )
    for load in loads:
        load.start()
    for load in loads:
        load.wait()
    for at in range(0, width, tile):
        gate_w, up_w, down_w = (held[:, k * width + at : k * width + at + tile] for k in range(3))
        gate_sum = jnp.dot(tok[...], gate_w, preferred_element_type=jnp.float32)
        up_sum = jnp.dot(tok[...], up_w, preferred_element_type=jnp.float32)
        back_sum = jnp.dot(grad[...], down_w, preferred_element_type=jnp.float32)
        logistic = jax.nn.sigmoid(gate_sum)
        act = gate_sum * logistic
        hid[:, at : at + tile] = (act * up_sum).astype(jnp.bfloat16)
        back[:, at : at + tile] = (
            back_sum * up_sum * logistic * (1.0 + gate_sum * (1.0 - logistic))
        ).astype(jnp.bfloat16)
        back[:, width + at : width + at + tile] = (back_sum * act).astype(jnp.bfloat16)
    keep = pltpu.make_async_copy(hid, hidden, hid_sem)
    keep.start()
    inv = 1.0 / total[0, 0]

    def term(left, right):
        out = lax.dot_general(
            left, right, (((0,), (0,)), ((), ())), preferred_element_type=jnp.float32
        )
        return (out * inv).astype(jnp.bfloat16)

    stores = []
    for y in range(NY):
        at = y * NX * per
        both = term(tok[:, at : at + NX * per], back[...])
        for x in range(NX):
            by_x[x, y, :, :width] = both[x * per : (x + 1) * per, width:]
            by_x[x, y, :, width:] = both[x * per : (x + 1) * per, :cut]
        stage[y, :, : width - cut] = both[:, cut:width]
        stage[y, :, width - cut :] = term(grad[:, at : at + NX * per], hid[...])
        stores.append(pltpu.make_async_copy(stage.at[y], by_y.at[y], out_sem.at[y]))
        stores[y].start()
    for store in stores:
        store.wait()
    keep.wait()


def add_x(got, out):
    acc = got[0].astype(jnp.float32)
    for i in range(1, NX):
        acc = acc + got[i].astype(jnp.float32)
    out[...] = acc.astype(jnp.bfloat16)


def turn(pos, part, *outs):
    for k, out in enumerate(outs):
        out[...] = part[(pos[1] + k) % NX]


def finish(from_y, *refs):
    parts, (gate, up, down) = refs[:NX], refs[NX:]
    acc = from_y[0].astype(jnp.float32)
    for i in range(1, NY):
        acc = acc + from_y[i].astype(jnp.float32)
    bcc = parts[0][...].astype(jnp.float32)
    for part in parts[1:]:
        bcc = bcc + part[...].astype(jnp.float32)
    width = up.shape[1]
    cut = acc.shape[1] - width
    up[...] = acc[:, :width]
    gate[:, :cut] = acc[:, width:]
    gate[:, cut:] = bcc[:, : width - cut]
    down[...] = bcc[:, width - cut :]


def a2a(value, axis):
    return lax.all_to_all(value, axis, split_axis=0, concat_axis=0, tiled=True)


def swap(value):
    return lax.ppermute(value, "c", [(0, 1), (1, 0)])


def along_z(value, by):
    return lax.ppermute(value, "z", [(i, (i + by) % NZ) for i in range(NZ)])


def step(
    tokens, out_grad, counts, block_moves, segment_ids, gate_weight, up_weight, down_weight
):
    bf = jnp.bfloat16
    f32 = jnp.float32
    slots, feat = tokens.shape
    per, hid = gate_weight.shape
    span = WORK * BLOCK
    model = 2 * NZ * feat
    weights = lax.all_gather(
        jnp.concatenate([gate_weight, up_weight, down_weight], axis=1), ROW, axis=0, tiled=True
    )
    pos = jnp.stack([lax.axis_index("y"), lax.axis_index("x"), counts[0], lax.axis_index("c"), lax.axis_index("z")])
    moves = block_moves.T
    box, work = pl.pallas_call(
        pack_x,
        out_shape=(
            jax.ShapeDtypeStruct((NX, 4 * BLOCK + NTAG, feat), bf),
            jax.ShapeDtypeStruct((2 * span, feat), bf),
        ),
        in_specs=[smem(), smem(), vmem(), vmem(), vmem()],
        out_specs=(vmem(), vmem()),
        scratch_shapes=[pltpu.VMEM((slots, feat), bf)],
        compiler_params=params(8),
        name="pack_x",
    )(pos, moves, segment_ids.reshape(CAP, BLOCK), tokens, out_grad)
    up2, down2 = along_z(work, 2), along_z(work, -2)
    up1, down1 = along_z(work, 1), along_z(work, -1)
    up3, down3, up4 = along_z(up2, 1), along_z(down2, -1), along_z(up2, 2)
    got = a2a(box, "x")
    box = pl.pallas_call(
        pack_y,
        out_shape=jax.ShapeDtypeStruct((NY, 2 * BLOCK + NTAG, feat), bf),
        in_specs=[smem(), smem(), vmem()],
        out_specs=vmem(),
        scratch_shapes=[pltpu.SMEM((NX,), jnp.int32)],
        compiler_params=params(8),
        name="pack_y",
    )(pos, moves, got)
    got = a2a(box, "y")
    box, total = pl.pallas_call(
        pick_arrival,
        out_shape=(
            jax.ShapeDtypeStruct((NZ, 2 * BLOCK, feat), bf),
            jax.ShapeDtypeStruct((8, BLOCK), f32),
        ),
        in_specs=[smem(), smem(), vmem()],
        out_specs=(vmem(), vmem()),
        compiler_params=params(8),
        name="pick_arrival",
    )(pos, moves, got)
    late = a2a(box, "z")
    pieces = (work, up1, up2, up3, up4, down3, down2, down1)
    mine = pl.pallas_call(
        gather_up,
        out_shape=jax.ShapeDtypeStruct((NZ, 2 * span + 2 * BLOCK, feat), bf),
        in_specs=[smem()] + [vmem()] * (NZ + 1),
        out_specs=vmem(),
        compiler_params=params(12),
        name="gather_up",
    )(pos, *pieces, late)
    other = swap(mine)
    tok, grad = pl.pallas_call(
        lay_out,
        out_shape=(
            jax.ShapeDtypeStruct((span, model), bf),
            jax.ShapeDtypeStruct((span, model), bf),
        ),
        in_specs=[smem(), smem(), vmem(), vmem()],
        out_specs=(vmem(), vmem()),
        compiler_params=params(14),
        name="lay_out",
    )(pos, moves, mine, other)

    hbm = pl.BlockSpec(memory_space=pltpu.HBM)
    wide_x, wide_y = hid + CUT, 2 * hid - CUT
    hidden, by_x, by_y = pl.pallas_call(
        compute,
        out_shape=(
            pltpu.HBM((span, hid), bf),
            pltpu.VMEM((NX, NY, per, wide_x), bf),
            pltpu.HBM((NY, NX * per, wide_y), bf),
        ),
        in_specs=[vmem(), hbm, hbm, hbm],
        out_specs=(hbm, vmem(), hbm),
        scratch_shapes=[
            pltpu.VMEM((span, model), bf),
            pltpu.VMEM((span, model), bf),
            pltpu.VMEM((model, 3 * hid), bf),
            pltpu.VMEM((span, hid), bf),
            pltpu.VMEM((span, 2 * hid), bf),
            pltpu.VMEM((NY, NX * per, wide_y), bf),
            pltpu.SemaphoreType.DMA((3,)),
            pltpu.SemaphoreType.DMA((NY,)),
            pltpu.SemaphoreType.DMA(()),
        ],
        compiler_params=params(36),
        name="compute",
    )(
        total,
        pltpu.with_memory_space_constraint(tok, pltpu.HBM),
        pltpu.with_memory_space_constraint(grad, pltpu.HBM),
        pltpu.with_memory_space_constraint(weights, pltpu.HBM),
    )

    part_y = lax.psum_scatter(
        by_y.reshape(NY * NX * per, wide_y), "y", scatter_dimension=0, tiled=True
    )
    part_x = pl.pallas_call(
        add_x,
        out_shape=jax.ShapeDtypeStruct((NY, per, wide_x), bf),
        in_specs=[vmem()],
        out_specs=vmem(),
        compiler_params=params(8),
        name="add_x",
    )(a2a(by_x, "x"))
    from_y = a2a(part_x, "y")
    turned = pl.pallas_call(
        turn,
        out_shape=tuple(jax.ShapeDtypeStruct((per, wide_y), bf) for _ in range(NX)),
        in_specs=[smem(), vmem()],
        out_specs=(vmem(),) * NX,
        compiler_params=params(8),
        name="turn",
    )(pos, part_y.reshape(NX, per, wide_y))
    from_x = [turned[0]] + [
        lax.ppermute(turned[k], "x", [(i, (i + k) % NX) for i in range(NX)]) for k in range(1, NX)
    ]
    gate_grad, up_grad, down_grad = pl.pallas_call(
        finish,
        out_shape=tuple(jax.ShapeDtypeStruct((per, hid), f32) for _ in range(3)),
        in_specs=[vmem()] * (NX + 1),
        out_specs=(vmem(), vmem(), vmem()),
        compiler_params=params(8),
        name="finish",
    )(from_y, *from_x)
    return (hidden, gate_grad, up_grad, down_grad)


def solution(mesh):
    torus = Mesh(mesh.devices.reshape(NY, NX, NZ, 2), ("y", "x", "z", "c"))
    return jax.shard_map(
        step,
        mesh=torus,
        in_specs=(P(ROW, COL), P(ROW, COL), P(ROW), P(), P(ROW), P(ROW, COL), P(ROW, COL), P(ROW, COL)),
        out_specs=(P(ROW, COL), P(ROW, COL), P(ROW, COL), P(ROW, COL)),
        check_vma=False,
    )
```

profile of v0, /device:TPU:94, one launch (start us, length us, event | category | flops | bytes accessed | tf_op | source)
XLA Modules:
  0.0 225.1 jit_solution(9334099370592432028)
XLA Ops:
  7.2 1.6 pad_maximum_fusion
  12.8 2.1 pack_x.1
  14.9 12.2 %all_to_all.25.got = bf16[4,528,128]{2,1,0:T(8,128)(2,1)S(1)} all-to-all(bf16[4,528,128]{2,1,0:T(8,128)(2,1)S(1)} %get-tuple-element.20), channel_id=1, replica_groups=mesh['y'=8,'x'=4,'z'=8,'c'=2] {'x'}, dimensions={0} | all-to-all | bytes 1081344 | tf_op jit(solution)/shard_map/all_to_all | solution.py:267
  28.0 25.6 %all_to_all.26.got = bf16[8,272,128]{2,1,0:T(8,128)(2,1)S(1)} all-to-all(bf16[8,272,128]{2,1,0:T(8,128)(2,1)S(1)} %pack_y.1), channel_id=1, replica_groups=mesh['y'=8,'x'=4,'z'=8,'c'=2] {'y'}, dimensions={0} | all-to-all | bytes 1114112 | tf_op jit(solution)/shard_map/all_to_all | solution.py:267
  53.5 1.6 pick_arrival.1
  55.2 9.4 %all-to-all-start.2 = ((bf16[8,256,128]{2,1,0:T(8,128)(2,1)}), bf16[8,256,128]{2,1,0:T(8,128)(2,1)S(1)}, u32[]{:S(2)}, u32[]{:S(2)}) async-start(bf16[8,256,128]{2,1,0:T(8,128)(2,1)} %get-tuple-element.23), calls=%async_computation.2 | async-start | bytes 1048576 | tf_op jit(solution)/shard_map/all_to_all | solution.py:267
  64.5 4.7 %collective-permute-start.4 = (bf16[1024,128]{1,0:T(8,128)(2,1)S(1)}, bf16[1024,128]{1,0:T(8,128)(2,1)S(1)}, u32[]{:S(2)}, u32[]{:S(2)}) collective-permute-start(bf16[1024,128]{1,0:T(8,128)(2,1)S(1)} %get-tuple-element.22.refs_0_), channel_id=1, source_target_pairs={{0,12},{2,14},{4,0},{6,2},{8,4},{10,6},{12,8},{14,10},{1,13},{3,15... | collective-permute-start | bytes 786440 | tf_op jit(solution)/shard_map/ppermute | solution.py:275
  69.2 2.2 collective-permute-start.1
  71.4 3.1 %collective-permute-start.6 = (bf16[1024,128]{1,0:T(8,128)(2,1)S(1)}, bf16[1024,128]{1,0:T(8,128)(2,1)S(1)}, u32[]{:S(2)}, u32[]{:S(2)}) collective-permute-start(bf16[1024,128]{1,0:T(8,128)(2,1)S(1)} %get-tuple-element.22.refs_0_), channel_id=1, source_target_pairs={{0,14},{2,0},{4,2},{6,4},{8,6},{10,8},{12,10},{14,12},{1,15},{3,1}... | collective-permute-start | bytes 786440 | tf_op jit(solution)/shard_map/ppermute | solution.py:275
  74.6 3.4 %collective-permute-start = (bf16[1024,128]{1,0:T(8,128)(2,1)S(1)}, bf16[1024,128]{1,0:T(8,128)(2,1)S(1)}, u32[]{:S(2)}, u32[]{:S(2)}) collective-permute-start(bf16[1024,128]{1,0:T(8,128)(2,1)S(1)} %get-tuple-element.22.refs_0_), channel_id=1, source_target_pairs={{0,2},{2,4},{4,6},{6,8},{8,10},{10,12},{12,14},{14,0},{1,3},{3,5},... | collective-permute-start | bytes 786440 | tf_op jit(solution)/shard_map/ppermute | solution.py:275
  77.9 12.2 %collective-permute-done.4.refs_6_ = bf16[1024,128]{1,0:T(8,128)(2,1)S(1)} collective-permute-done((bf16[1024,128]{1,0:T(8,128)(2,1)S(1)}, bf16[1024,128]{1,0:T(8,128)(2,1)S(1)}, u32[]{:S(2)}, u32[]{:S(2)}) %collective-permute-start.4) | collective-permute-done | bytes 262176 | tf_op jit(solution)/shard_map/ppermute | solution.py:275
  90.1 1.9 collective-permute-start.5
  92.0 5.1 %collective-permute-start.3 = (bf16[1024,128]{1,0:T(8,128)(2,1)S(1)}, bf16[1024,128]{1,0:T(8,128)(2,1)S(1)}, u32[]{:S(2)}, u32[]{:S(2)}) collective-permute-start(bf16[1024,128]{1,0:T(8,128)(2,1)S(1)} %collective-permute-done.1.refs_2_), channel_id=1, source_target_pairs={{0,4},{2,6},{4,8},{6,10},{8,12},{10,14},{12,0},{14,2},{1,5},{3,7},... | collective-permute-start | bytes 786440 | tf_op jit(solution)/shard_map/ppermute | solution.py:275
  97.2 4.1 %collective-permute-start.2 = (bf16[1024,128]{1,0:T(8,128)(2,1)S(1)}, bf16[1024,128]{1,0:T(8,128)(2,1)S(1)}, u32[]{:S(2)}, u32[]{:S(2)}) collective-permute-start(bf16[1024,128]{1,0:T(8,128)(2,1)S(1)} %collective-permute-done.1.refs_2_), channel_id=1, source_target_pairs={{0,2},{2,4},{4,6},{6,8},{8,10},{10,12},{12,14},{14,0},{1,3},{3,5},... | collective-permute-start | bytes 786440 | tf_op jit(solution)/shard_map/ppermute | solution.py:275
  101.3 5.4 %collective-permute-done.3.refs_4_ = bf16[1024,128]{1,0:T(8,128)(2,1)S(1)} collective-permute-done((bf16[1024,128]{1,0:T(8,128)(2,1)S(1)}, bf16[1024,128]{1,0:T(8,128)(2,1)S(1)}, u32[]{:S(2)}, u32[]{:S(2)}) %collective-permute-start.3) | collective-permute-done | bytes 262176 | tf_op jit(solution)/shard_map/ppermute | solution.py:275
  106.7 1.5 collective-permute-done.2.refs_3_
  108.9 1.9 collective-permute-start.7
  110.9 4.9 %collective-permute-done.7.other = bf16[8,1280,128]{2,1,0:T(8,128)(2,1)S(1)} collective-permute-done((bf16[8,1280,128]{2,1,0:T(8,128)(2,1)S(1)}, bf16[8,1280,128]{2,1,0:T(8,128)(2,1)S(1)}, u32[]{:S(2)}, u32[]{:S(2)}) %collective-permute-start.7) | collective-permute-done | bytes 2621472 | tf_op jit(solution)/shard_map/ppermute | solution.py:271
  115.7 2.6 %lay_out.1 = (bf16[512,2048]{1,0:T(8,128)(2,1)S(1)}, bf16[512,2048]{1,0:T(8,128)(2,1)S(1)}) custom-call(s32[5]{0:T(128)S(1)} %stack.19.pos, s32[3,16]{1,0:T(4,128)S(1)} %bitcast.12, bf16[8,1280,128]{2,1,0:T(8,128)(2,1)S(1)} %gather_up.1.mine, bf16[8,1280,128]{2,1,0:T(8,128)(2,1)S(1)} %collective-permute-done.7.other), custom_call_target="tpu_custom_call" | custom-call | tf_op jit(solution)/shard_map/lay_out/pallas_call | solution.py:340
  118.4 1.3 copy-done
  119.7 1.3 copy-done.1
  121.0 11.9 %compute.1 = (bf16[512,512]{1,0:T(8,128)(2,1)}, bf16[4,8,64,640]{3,2,1,0:T(8,128)(2,1)S(1)}, bf16[8,256,896]{2,1,0:T(8,128)(2,1)}) custom-call(f32[8,128]{1,0:T(8,128)S(1)} %get-tuple-element.21.total, bf16[512,2048]{1,0:T(8,128)(2,1)} %copy-done, bf16[512,2048]{1,0:T(8,128)(2,1)} %copy-done.1, bf16[2048,1536]{1,0:T(8,128)(2,1)} %all-gather.2.cloned.1.call-done.weights), custom_call_target="tpu_custom_call" | custom-call | tf_op jit(solution)/shard_map/compute/pallas_call | solution.py:354
  132.9 36.6 %all_to_all.27.got = bf16[4,8,64,640]{3,2,1,0:T(8,128)(2,1)S(1)} all-to-all(bf16[4,8,64,640]{3,2,1,0:T(8,128)(2,1)S(1)} %get-tuple-element.27), channel_id=1, replica_groups=mesh['y'=8,'x'=4,'z'=8,'c'=2] {'x'}, dimensions={0} | all-to-all | bytes 5242880 | tf_op jit(solution)/shard_map/all_to_all | solution.py:267
  169.5 1.2 add_x.1
  170.7 5.4 %all-to-all-start.4 = ((bf16[8,64,640]{2,1,0:T(8,128)(2,1)}), bf16[8,64,640]{2,1,0:T(8,128)(2,1)S(1)}, u32[]{:S(2)}, u32[]{:S(2)}) async-start(bf16[8,64,640]{2,1,0:T(8,128)(2,1)} %add_x.1), calls=%async_computation.4 | async-start | bytes 1310720 | tf_op jit(solution)/shard_map/all_to_all | solution.py:267
  176.1 24.8 %reduce-scatter.2.cloned.1.call-done = bf16[256,896]{1,0:T(8,128)(2,1)} async-done(((bf16[2048,896]{1,0:T(8,128)(2,1)}), bf16[256,896]{1,0:T(8,128)(2,1)}) %reduce-scatter.2.cloned.1.call-update) | async-done | bytes 458768 | tf_op jit(solution)/shard_map/reduce_scatter | solution.py:383
  200.9 1.0 copy-done.2
  202.5 1.9 collective-permute-start.8
  204.4 5.1 %collective-permute-start.9 = (bf16[64,896]{1,0:T(8,128)(2,1)S(1)}, bf16[64,896]{1,0:T(8,128)(2,1)S(1)}, u32[]{:S(2)}, u32[]{:S(2)}) collective-permute-start(bf16[64,896]{1,0:T(8,128)(2,1)S(1)} %get-tuple-element.31), channel_id=1, source_target_pairs={{0,32},{16,48},{32,0},{48,16},{1,33},{17,49},{33,1},{49,17},{2,34}... | collective-permute-start | bytes 344072 | tf_op jit(solution)/shard_map/ppermute | solution.py:404
  209.6 1.9 collective-permute-start.10
  211.5 1.5 collective-permute-done.9.refs_2_
  213.0 4.4 %collective-permute-done.10.refs_3_ = bf16[64,896]{1,0:T(8,128)(2,1)S(1)} collective-permute-done((bf16[64,896]{1,0:T(8,128)(2,1)S(1)}, bf16[64,896]{1,0:T(8,128)(2,1)S(1)}, u32[]{:S(2)}, u32[]{:S(2)}) %collective-permute-start.10) | collective-permute-done | bytes 114720 | tf_op jit(solution)/shard_map/ppermute | solution.py:404
  (30 shorter events, 6.4 us)
Async XLA Ops:
  7.2 113.9 %all-gather.2.cloned.1.call-start = ((), (), s32[]{:S(2)}) async-start(), calls=%async_computation.6 | async-start | bytes 6488064 | tf_op jit(solution)/shard_map/all_gather | solution.py:287
  9.6 0.9 copy-start.3
  10.5 0.9 copy-start.4
  11.4 0.7 copy-start.5
  12.1 0.7 copy-start.7
  55.2 53.0 %all-to-all-start.2 = ((bf16[8,256,128]{2,1,0:T(8,128)(2,1)}), bf16[8,256,128]{2,1,0:T(8,128)(2,1)S(1)}, u32[]{:S(2)}, u32[]{:S(2)}) async-start(bf16[8,256,128]{2,1,0:T(8,128)(2,1)} %get-tuple-element.23), calls=%async_computation.2 | async-start | bytes 1048576 | tf_op jit(solution)/shard_map/all_to_all | solution.py:267
  64.5 136.4 %reduce-scatter.2.cloned.1.call-start = ((), (), s32[]{:S(2)}) async-start(), calls=%async_computation.7 | async-start | bytes 4128768 | tf_op jit(solution)/shard_map/reduce_scatter | solution.py:383
  64.5 51.2 %copy-start.6 = (s32[16,3]{0,1:T(4,128)S(1)}, s32[16,3]{0,1:T(4,128)}, u32[]{:S(2)}) copy-start(s32[16,3]{0,1:T(4,128)} %param.11) | copy-start | bytes 580
  64.5 25.6 %collective-permute-start.4 = (bf16[1024,128]{1,0:T(8,128)(2,1)S(1)}, bf16[1024,128]{1,0:T(8,128)(2,1)S(1)}, u32[]{:S(2)}, u32[]{:S(2)}) collective-permute-start(bf16[1024,128]{1,0:T(8,128)(2,1)S(1)} %get-tuple-element.22.refs_0_), channel_id=1, source_target_pairs={{0,12},{2,14},{4,0},{6,2},{8,4},{10,6},{12,8},{14,10},{1,13},{3,15... | collective-permute-start | bytes 786440 | tf_op jit(solution)/shard_map/ppermute | solution.py:275
  69.2 22.8 %collective-permute-start.1 = (bf16[1024,128]{1,0:T(8,128)(2,1)S(1)}, bf16[1024,128]{1,0:T(8,128)(2,1)S(1)}, u32[]{:S(2)}, u32[]{:S(2)}) collective-permute-start(bf16[1024,128]{1,0:T(8,128)(2,1)S(1)} %get-tuple-element.22.refs_0_), channel_id=1, source_target_pairs={{0,4},{2,6},{4,8},{6,10},{8,12},{10,14},{12,0},{14,2},{1,5},{3,7},... | collective-permute-start | bytes 786440 | tf_op jit(solution)/shard_map/ppermute | solution.py:275
  71.4 29.8 %collective-permute-start.6 = (bf16[1024,128]{1,0:T(8,128)(2,1)S(1)}, bf16[1024,128]{1,0:T(8,128)(2,1)S(1)}, u32[]{:S(2)}, u32[]{:S(2)}) collective-permute-start(bf16[1024,128]{1,0:T(8,128)(2,1)S(1)} %get-tuple-element.22.refs_0_), channel_id=1, source_target_pairs={{0,14},{2,0},{4,2},{6,4},{8,6},{10,8},{12,10},{14,12},{1,15},{3,1}... | collective-permute-start | bytes 786440 | tf_op jit(solution)/shard_map/ppermute | solution.py:275
  74.6 26.7 %collective-permute-start = (bf16[1024,128]{1,0:T(8,128)(2,1)S(1)}, bf16[1024,128]{1,0:T(8,128)(2,1)S(1)}, u32[]{:S(2)}, u32[]{:S(2)}) collective-permute-start(bf16[1024,128]{1,0:T(8,128)(2,1)S(1)} %get-tuple-element.22.refs_0_), channel_id=1, source_target_pairs={{0,2},{2,4},{4,6},{6,8},{8,10},{10,12},{12,14},{14,0},{1,3},{3,5},... | collective-permute-start | bytes 786440 | tf_op jit(solution)/shard_map/ppermute | solution.py:275
  90.1 11.1 %collective-permute-start.5 = (bf16[1024,128]{1,0:T(8,128)(2,1)S(1)}, bf16[1024,128]{1,0:T(8,128)(2,1)S(1)}, u32[]{:S(2)}, u32[]{:S(2)}) collective-permute-start(bf16[1024,128]{1,0:T(8,128)(2,1)S(1)} %collective-permute-done.4.refs_6_), channel_id=1, source_target_pairs={{0,14},{2,0},{4,2},{6,4},{8,6},{10,8},{12,10},{14,12},{1,15},{3,1}... | collective-permute-start | bytes 786440 | tf_op jit(solution)/shard_map/ppermute | solution.py:275
  92.0 14.6 %collective-permute-start.3 = (bf16[1024,128]{1,0:T(8,128)(2,1)S(1)}, bf16[1024,128]{1,0:T(8,128)(2,1)S(1)}, u32[]{:S(2)}, u32[]{:S(2)}) collective-permute-start(bf16[1024,128]{1,0:T(8,128)(2,1)S(1)} %collective-permute-done.1.refs_2_), channel_id=1, source_target_pairs={{0,4},{2,6},{4,8},{6,10},{8,12},{10,14},{12,0},{14,2},{1,5},{3,7},... | collective-permute-start | bytes 786440 | tf_op jit(solution)/shard_map/ppermute | solution.py:275
  97.2 11.1 %collective-permute-start.2 = (bf16[1024,128]{1,0:T(8,128)(2,1)S(1)}, bf16[1024,128]{1,0:T(8,128)(2,1)S(1)}, u32[]{:S(2)}, u32[]{:S(2)}) collective-permute-start(bf16[1024,128]{1,0:T(8,128)(2,1)S(1)} %collective-permute-done.1.refs_2_), channel_id=1, source_target_pairs={{0,2},{2,4},{4,6},{6,8},{8,10},{10,12},{12,14},{14,0},{1,3},{3,5},... | collective-permute-start | bytes 786440 | tf_op jit(solution)/shard_map/ppermute | solution.py:275
  108.9 6.8 %collective-permute-start.7 = (bf16[8,1280,128]{2,1,0:T(8,128)(2,1)S(1)}, bf16[8,1280,128]{2,1,0:T(8,128)(2,1)S(1)}, u32[]{:S(2)}, u32[]{:S(2)}) collective-permute-start(bf16[8,1280,128]{2,1,0:T(8,128)(2,1)S(1)} %gather_up.1.mine), channel_id=1, source_target_pairs={{0,1},{1,0},{2,3},{3,2},{4,5},{5,4},{6,7},{7,6},{8,9},{9,8},{10,11... | collective-permute-start | bytes 7864328 | tf_op jit(solution)/shard_map/ppermute | solution.py:271
  118.4 1.3 copy-start
  119.7 1.3 copy-start.1
  170.7 40.8 %all-to-all-start.4 = ((bf16[8,64,640]{2,1,0:T(8,128)(2,1)}), bf16[8,64,640]{2,1,0:T(8,128)(2,1)S(1)}, u32[]{:S(2)}, u32[]{:S(2)}) async-start(bf16[8,64,640]{2,1,0:T(8,128)(2,1)} %add_x.1), calls=%async_computation.4 | async-start | bytes 1310720 | tf_op jit(solution)/shard_map/all_to_all | solution.py:267
  200.9 1.0 copy-start.2
  202.5 9.0 %collective-permute-start.8 = (bf16[64,896]{1,0:T(8,128)(2,1)S(1)}, bf16[64,896]{1,0:T(8,128)(2,1)S(1)}, u32[]{:S(2)}, u32[]{:S(2)}) collective-permute-start(bf16[64,896]{1,0:T(8,128)(2,1)S(1)} %get-tuple-element.30), channel_id=1, source_target_pairs={{0,16},{16,32},{32,48},{48,0},{1,17},{17,33},{33,49},{49,1},{2,18}... | collective-permute-start | bytes 344072 | tf_op jit(solution)/shard_map/ppermute | solution.py:404
  204.4 8.6 %collective-permute-start.9 = (bf16[64,896]{1,0:T(8,128)(2,1)S(1)}, bf16[64,896]{1,0:T(8,128)(2,1)S(1)}, u32[]{:S(2)}, u32[]{:S(2)}) collective-permute-start(bf16[64,896]{1,0:T(8,128)(2,1)S(1)} %get-tuple-element.31), channel_id=1, source_target_pairs={{0,32},{16,48},{32,0},{48,16},{1,33},{17,49},{33,1},{49,17},{2,34}... | collective-permute-start | bytes 344072 | tf_op jit(solution)/shard_map/ppermute | solution.py:404
  209.6 7.9 %collective-permute-start.10 = (bf16[64,896]{1,0:T(8,128)(2,1)S(1)}, bf16[64,896]{1,0:T(8,128)(2,1)S(1)}, u32[]{:S(2)}, u32[]{:S(2)}) collective-permute-start(bf16[64,896]{1,0:T(8,128)(2,1)S(1)} %get-tuple-element.32), channel_id=1, source_target_pairs={{0,48},{16,0},{32,16},{48,32},{1,49},{17,1},{33,17},{49,33},{2,50}... | collective-permute-start | bytes 344072 | tf_op jit(solution)/shard_map/ppermute | solution.py:404
Sparse Core Ops, SparseCore 0:
  11.1 97.7 all-gather.1
  133.0 67.7 reduce-scatter.1
where the time goes:
time: 226 us; the launch traced here: 225 us
  blocking collectives  74.3 us (33%)
  waiting for transfers between devices  54.8 us (24%)
  starting transfers between devices  50.1 us (22%)
  Pallas kernels  22.4 us (10%)
  between operations  14.9 us (7%)
  local copies, waits for them, and re-layouts  6.97 us (3%)
    all_to_all x3, blocking collectives, a2a(): return lax.all_to_all(value, axis, split_axis=0, concat_axis=0, tiled=True)  74.3 us
    reduce_scatter x1, waiting for transfers between devices, step(): lax.psum_scatter(by_y.reshape(NY * NX * per, wide_y), 'y', scatter_dimens...  24.8 us
    ppermute x7, starting transfers between devices, along_z(): return lax.ppermute(value, 'z', [(i, (i + by) % NZ) for i in range(NZ)])  24.4 us
    ppermute x7, waiting for transfers between devices, along_z(): return lax.ppermute(value, 'z', [(i, (i + by) % NZ) for i in range(NZ)])  19.1 us
    all_to_all x2, starting transfers between devices, a2a(): return lax.all_to_all(value, axis, split_axis=0, concat_axis=0, tiled=True)  14.8 us
    pallas_call x1, Pallas kernels, step(): pl.pallas_call(compute, out_shape=(pltpu.HBM((span, hid), bf), pltpu.VMEM...  11.9 us
    ppermute x3, starting transfers between devices, step(): lax.ppermute(turned[k], 'x', [(i, (i + k) % NX) for i in range(NX)])  8.97 us
    unnamed x16, local copies, waits for them, and re-layouts  6.89 us
  transfers between devices with their start and end apart: 15, of which 7 were waited for; matrix products, arithmetic and copies ran while one was open for 0% of the time, Pallas kernels for 4%

commit v1 on v0

--- a/solution.py
+++ b/solution.py
@@ -14,7 +14,7 @@
 ROW = ("y", "x")
 COL = ("z", "c")
 NTAG = 16
-CUT = 128
+CUT = 256
 
 
 def vmem():
@@ -131,15 +131,13 @@
         box[d] = got[sy, : 2 * BLOCK, :]
 
 
-def gather_up(pos, *refs):
-    pieces, late, out = refs[:NZ], refs[NZ], refs[NZ + 1]
-    rows = pieces[0].shape[0]
-    for k, piece in enumerate(pieces):
-        out[k, :rows, :] = piece[...]
-        out[k, rows:, :] = late[(pos[4] - k + NZ) % NZ]
-
-
-def lay_out(pos, moves, mine, other, tok, grad):
+def gather_up(*refs):
+    out = refs[-1]
+    for k, piece in enumerate(refs[:-1]):
+        out[k] = piece[...]
+
+
+def lay_out(pos, moves, mine, other, late, late_other, tok_out, grad_out, tok, grad, sems):
     me = pos[0] * NX + pos[1]
     first = pos[3] == 0
     my_z = pos[4]
@@ -157,27 +155,30 @@
 
     nth = lax.fori_loop(0, CAP, own, 0)
     here = lax.fori_loop(0, move_count(moves), came, 0)
-
-    def pick(z, side, low, size):
+    there = (here == 1) & (nth < WORK)
+    rows = pl.ds(pl.multiple_of(jnp.minimum(nth, WORK - 1) * BLOCK, BLOCK), BLOCK)
+    sends = []
+    for z in range(NZ):
         away = (my_z - z + NZ) % NZ
-        take = first if side == 0 else jnp.logical_not(first)
-        rows = slice(low, low + size)
-        return jnp.where(take, mine[away, rows, :], other[away, rows, :])
-
-    for z in range(NZ):
         for side in range(2):
             cols = slice((2 * z + side) * BLOCK, (2 * z + side + 1) * BLOCK)
-            tok[:, cols] = pick(z, side, 0, span)
-            grad[:, cols] = pick(z, side, span, span)
-
-    @pl.when((here == 1) & (nth < WORK))
-    def _():
-        rows = pl.ds(pl.multiple_of(nth * BLOCK, BLOCK), BLOCK)
-        for z in range(NZ):
-            for side in range(2):
-                cols = slice((2 * z + side) * BLOCK, (2 * z + side + 1) * BLOCK)
-                tok[rows, cols] = pick(z, side, 2 * span, BLOCK)
-                grad[rows, cols] = pick(z, side, 2 * span + BLOCK, BLOCK)
+            take = first if side == 0 else jnp.logical_not(first)
+            block = jnp.where(take, mine[away], other[away])
+            tok[:, cols] = block[:span]
+            grad[:, cols] = block[span:]
+
+            @pl.when(there)
+            def _():
+                extra = jnp.where(take, late[z], late_other[z])
+                tok[rows, cols] = extra[:BLOCK]
+                grad[rows, cols] = extra[BLOCK:]
+
+        both = slice(2 * z * BLOCK, 2 * (z + 1) * BLOCK)
+        for k, (ref, out) in enumerate(((tok, tok_out), (grad, grad_out))):
+            sends.append(pltpu.make_async_copy(ref.at[:, both], out.at[:, both], sems.at[k, z]))
+            sends[-1].start()
+    for send in sends:
+        send.wait()
 
 
 def compute(
@@ -188,19 +189,24 @@
     tile = width // 2
     per = by_x.shape[2]
     cut = by_x.shape[3] - width
+    fore = 2 * width
     loads = (
         pltpu.make_async_copy(tok_in, tok, in_sem.at[0]),
-        pltpu.make_async_copy(grad_in, grad, in_sem.at[1]),
-        pltpu.make_async_copy(weights, held, in_sem.at[2]),
+        pltpu.make_async_copy(weights.at[:, :fore], held.at[:, :fore], in_sem.at[1]),
+        pltpu.make_async_copy(grad_in, grad, in_sem.at[2]),
+        pltpu.make_async_copy(weights.at[:, fore:], held.at[:, fore:], in_sem.at[3]),
     )
     for load in loads:
         load.start()
-    for load in loads:
-        load.wait()
+    loads[0].wait()
+    loads[1].wait()
+    sums = jnp.dot(tok[...], held[:, :fore], preferred_element_type=jnp.float32)
+    loads[2].wait()
+    loads[3].wait()
     for at in range(0, width, tile):
-        gate_w, up_w, down_w = (held[:, k * width + at : k * width + at + tile] for k in range(3))
-        gate_sum = jnp.dot(tok[...], gate_w, preferred_element_type=jnp.float32)
-        up_sum = jnp.dot(tok[...], up_w, preferred_element_type=jnp.float32)
+        gate_sum = sums[:, at : at + tile]
+        up_sum = sums[:, width + at : width + at + tile]
+        down_w = held[:, fore + at : fore + at + tile]
         back_sum = jnp.dot(grad[...], down_w, preferred_element_type=jnp.float32)
         logistic = jax.nn.sigmoid(gate_sum)
         act = gate_sum * logistic
@@ -330,26 +336,28 @@
     pieces = (work, up1, up2, up3, up4, down3, down2, down1)
     mine = pl.pallas_call(
         gather_up,
-        out_shape=jax.ShapeDtypeStruct((NZ, 2 * span + 2 * BLOCK, feat), bf),
-        in_specs=[smem()] + [vmem()] * (NZ + 1),
+        out_shape=jax.ShapeDtypeStruct((NZ, 2 * span, feat), bf),
+        in_specs=[vmem()] * NZ,
         out_specs=vmem(),
         compiler_params=params(12),
         name="gather_up",
-    )(pos, *pieces, late)
+    )(*pieces)
     other = swap(mine)
+    hbm = pl.BlockSpec(memory_space=pltpu.HBM)
     tok, grad = pl.pallas_call(
         lay_out,
-        out_shape=(
-            jax.ShapeDtypeStruct((span, model), bf),
-            jax.ShapeDtypeStruct((span, model), bf),
-        ),
-        in_specs=[smem(), smem(), vmem(), vmem()],
-        out_specs=(vmem(), vmem()),
+        out_shape=(pltpu.HBM((span, model), bf), pltpu.HBM((span, model), bf)),
+        in_specs=[smem(), smem(), vmem(), vmem(), vmem(), vmem()],
+        out_specs=(hbm, hbm),
+        scratch_shapes=[
+            pltpu.VMEM((span, model), bf),
+            pltpu.VMEM((span, model), bf),
+            pltpu.SemaphoreType.DMA((2, NZ)),
+        ],
         compiler_params=params(14),
         name="lay_out",
-    )(pos, moves, mine, other)
-
-    hbm = pl.BlockSpec(memory_space=pltpu.HBM)
+    )(pos, moves, mine, other, late, swap(late))
+
     wide_x, wide_y = hid + CUT, 2 * hid - CUT
     hidden, by_x, by_y = pl.pallas_call(
         compute,
@@ -367,7 +375,7 @@
             pltpu.VMEM((span, hid), bf),
             pltpu.VMEM((span, 2 * hid), bf),
             pltpu.VMEM((NY, NX * per, wide_y), bf),
-            pltpu.SemaphoreType.DMA((3,)),
+            pltpu.SemaphoreType.DMA((4,)),
             pltpu.SemaphoreType.DMA((NY,)),
             pltpu.SemaphoreType.DMA(()),
         ],

time: 226 us -> 200 us (0.88)
  the two profiles are of different devices: /device:TPU:94 before, /device:TPU:1 now
where the time goes in v1:
time: 200 us; the launch traced here: 199 us
  starting transfers between devices  64.4 us (32%)
  blocking collectives  58.7 us (29%)
  waiting for transfers between devices  29.7 us (15%)
  Pallas kernels  24.4 us (12%)
  between operations  14.9 us (7%)
  local copies, waits for them, and re-layouts  4.98 us (2%)
    all_to_all x2, blocking collectives, a2a(): return lax.all_to_all(value, axis, split_axis=0, concat_axis=0, tiled=True)  58.7 us
    ppermute x7, starting transfers between devices, along_z(): return lax.ppermute(value, 'z', [(i, (i + by) % NZ) for i in range(NZ)])  29.8 us
    all_to_all x3, starting transfers between devices, a2a(): return lax.all_to_all(value, axis, split_axis=0, concat_axis=0, tiled=True)  17.6 us
    ppermute x7, waiting for transfers between devices, along_z(): return lax.ppermute(value, 'z', [(i, (i + by) % NZ) for i in range(NZ)])  15.4 us
    pallas_call x1, Pallas kernels, step(): pl.pallas_call(compute, out_shape=(pltpu.HBM((span, hid), bf), pltpu.VMEM...  10.9 us
    all_to_all x3, waiting for transfers between devices, a2a(): return lax.all_to_all(value, axis, split_axis=0, concat_axis=0, tiled=True)  10.6 us
    ppermute x3, starting transfers between devices, step(): lax.ppermute(turned[k], 'x', [(i, (i + k) % NX) for i in range(NX)])  9.84 us
    ppermute x2, starting transfers between devices, swap(): return lax.ppermute(value, 'c', [(0, 1), (1, 0)])  7.09 us
  transfers between devices with their start and end apart: 17, of which 5 were waited for; matrix products, arithmetic and copies ran while one was open for 0% of the time, Pallas kernels for 6%

profile of v1, /device:TPU:1, one launch (start us, length us, event | category | flops | bytes accessed | tf_op | source)
XLA Modules:
  0.0 198.7 jit_solution(6727268552470671030)
XLA Ops:
  7.2 1.6 pad_maximum_fusion
  9.6 0.9 copy-done.1
  10.5 0.9 copy-done.2
  12.8 2.9 %pack_x.1 = (bf16[4,528,128]{2,1,0:T(8,128)(2,1)}, bf16[1024,128]{1,0:T(8,128)(2,1)S(1)}) custom-call(s32[5]{0:T(128)S(1)} %stack.19.pos, s32[3,16]{1,0:T(4,128)S(1)} %bitcast.9, s32[6,128]{1,0:T(8,128)S(1)} %bitcast.13, bf16[768,128]{1,0:T(8,128)(2,1)S(1)} %copy-done.1, bf16[768,128]{1,0:T(8,128)(2,1)S(1)} %copy-done.2), custom_call_target="tpu_custom_call" | custom-call | tf_op jit(solution)/shard_map/pack_x/pallas_call | solution.py:298
  15.7 4.9 %all-to-all-start = ((bf16[4,528,128]{2,1,0:T(8,128)(2,1)}), bf16[4,528,128]{2,1,0:T(8,128)(2,1)S(1)}, u32[]{:S(2)}, u32[]{:S(2)}) async-start(bf16[4,528,128]{2,1,0:T(8,128)(2,1)} %get-tuple-element.20), calls=%async_computation | async-start | bytes 1081344 | tf_op jit(solution)/shard_map/all_to_all | solution.py:273
  20.7 10.6 %collective-permute-start.4 = (bf16[1024,128]{1,0:T(8,128)(2,1)S(1)}, bf16[1024,128]{1,0:T(8,128)(2,1)S(1)}, u32[]{:S(2)}, u32[]{:S(2)}) collective-permute-start(bf16[1024,128]{1,0:T(8,128)(2,1)S(1)} %get-tuple-element.22.refs_0_), channel_id=1, source_target_pairs={{0,12},{2,14},{4,0},{6,2},{8,4},{10,6},{12,8},{14,10},{1,13},{3,15... | collective-permute-start | bytes 786440 | tf_op jit(solution)/shard_map/ppermute | solution.py:281
  31.3 1.9 collective-permute-start.1
  34.0 1.8 pack_y.1
  35.7 6.8 %all-to-all-start.1 = ((bf16[8,272,128]{2,1,0:T(8,128)(2,1)}), bf16[8,272,128]{2,1,0:T(8,128)(2,1)S(1)}, u32[]{:S(2)}, u32[]{:S(2)}) async-start(bf16[8,272,128]{2,1,0:T(8,128)(2,1)} %pack_y.1), calls=%async_computation.1 | async-start | bytes 1114112 | tf_op jit(solution)/shard_map/all_to_all | solution.py:273
  42.6 6.9 %collective-permute-start.6 = (bf16[1024,128]{1,0:T(8,128)(2,1)S(1)}, bf16[1024,128]{1,0:T(8,128)(2,1)S(1)}, u32[]{:S(2)}, u32[]{:S(2)}) collective-permute-start(bf16[1024,128]{1,0:T(8,128)(2,1)S(1)} %get-tuple-element.22.refs_0_), channel_id=1, source_target_pairs={{0,14},{2,0},{4,2},{6,4},{8,6},{10,8},{12,10},{14,12},{1,15},{3,1}... | collective-permute-start | bytes 786440 | tf_op jit(solution)/shard_map/ppermute | solution.py:281
  49.5 1.9 collective-permute-start
  51.4 4.6 %collective-permute-start.5 = (bf16[1024,128]{1,0:T(8,128)(2,1)S(1)}, bf16[1024,128]{1,0:T(8,128)(2,1)S(1)}, u32[]{:S(2)}, u32[]{:S(2)}) collective-permute-start(bf16[1024,128]{1,0:T(8,128)(2,1)S(1)} %collective-permute-done.4.refs_6_), channel_id=1, source_target_pairs={{0,14},{2,0},{4,2},{6,4},{8,6},{10,8},{12,10},{14,12},{1,15},{3,1}... | collective-permute-start | bytes 786440 | tf_op jit(solution)/shard_map/ppermute | solution.py:281
  56.0 1.9 collective-permute-start.3
  57.9 1.9 collective-permute-start.2
  59.9 9.4 %collective-permute-done.3.refs_4_ = bf16[1024,128]{1,0:T(8,128)(2,1)S(1)} collective-permute-done((bf16[1024,128]{1,0:T(8,128)(2,1)S(1)}, bf16[1024,128]{1,0:T(8,128)(2,1)S(1)}, u32[]{:S(2)}, u32[]{:S(2)}) %collective-permute-start.3) | collective-permute-done | bytes 262176 | tf_op jit(solution)/shard_map/ppermute | solution.py:281
  69.3 6.1 %collective-permute-done.2.refs_3_ = bf16[1024,128]{1,0:T(8,128)(2,1)S(1)} collective-permute-done((bf16[1024,128]{1,0:T(8,128)(2,1)S(1)}, bf16[1024,128]{1,0:T(8,128)(2,1)S(1)}, u32[]{:S(2)}, u32[]{:S(2)}) %collective-permute-start.2) | collective-permute-done | bytes 262176 | tf_op jit(solution)/shard_map/ppermute | solution.py:281
  75.5 4.8 %collective-permute-start.7 = (bf16[8,1024,128]{2,1,0:T(8,128)(2,1)S(1)}, bf16[8,1024,128]{2,1,0:T(8,128)(2,1)}, u32[]{:S(2)}, u32[]{:S(2)}) collective-permute-start(bf16[8,1024,128]{2,1,0:T(8,128)(2,1)S(1)} %gather_up.1.mine), channel_id=1, source_target_pairs={{0,1},{1,0},{2,3},{3,2},{4,5},{5,4},{6,7},{7,6},{8,9},{9,8},{10,11... | collective-permute-start | bytes 6291464 | tf_op jit(solution)/shard_map/ppermute | solution.py:277
  80.3 0.8 pick_arrival.1
  81.1 20.4 %all_to_all.25.late = bf16[8,256,128]{2,1,0:T(8,128)(2,1)S(1)} all-to-all(bf16[8,256,128]{2,1,0:T(8,128)(2,1)S(1)} %get-tuple-element.23), channel_id=1, replica_groups=mesh['y'=8,'x'=4,'z'=8,'c'=2] {'z'}, dimensions={0} | all-to-all | bytes 1048576 | tf_op jit(solution)/shard_map/all_to_all | solution.py:273
  101.5 2.3 %collective-permute-start.8 = (bf16[8,256,128]{2,1,0:T(8,128)(2,1)S(1)}, bf16[8,256,128]{2,1,0:T(8,128)(2,1)S(1)}, u32[]{:S(2)}, u32[]{:S(2)}) collective-permute-start(bf16[8,256,128]{2,1,0:T(8,128)(2,1)S(1)} %all_to_all.25.late), channel_id=1, source_target_pairs={{0,1},{1,0},{2,3},{3,2},{4,5},{5,4},{6,7},{7,6},{8,9},{9,8},{10,11... | collective-permute-start | bytes 1572872 | tf_op jit(solution)/shard_map/ppermute | solution.py:277
  103.9 1.5 collective-permute-done.8.late_other
  105.4 5.2 %lay_out.1 = (bf16[512,2048]{1,0:T(8,128)(2,1)}, bf16[512,2048]{1,0:T(8,128)(2,1)}) custom-call(s32[5]{0:T(128)S(1)} %stack.19.pos, s32[3,16]{1,0:T(4,128)S(1)} %bitcast.12, bf16[8,1024,128]{2,1,0:T(8,128)(2,1)S(1)} %gather_up.1.mine, bf16[8,1024,128]{2,1,0:T(8,128)(2,1)} %collective-permute-done.7.other, bf16[8,256,128]{2,1,0:T(8,128)(2,1)S(1)} %all_to_all.25.late, ...), custom_call_target="tpu_custom_call" | custom-call | tf_op jit(solution)/shard_map/lay_out/pallas_call | solution.py:347
  110.5 2.2 %all-gather.2.cloned.1.call-done.weights = bf16[2048,1536]{1,0:T(8,128)(2,1)} async-done(((bf16[64,1536]{1,0:T(8,128)(2,1)}), bf16[2048,1536]{1,0:T(8,128)(2,1)}) %all-gather.2.cloned.1.call-update) | async-done | bytes 6291472 | tf_op jit(solution)/shard_map/all_gather | solution.py:293
  112.7 10.9 %compute.1 = (bf16[512,512]{1,0:T(8,128)(2,1)}, bf16[4,8,64,768]{3,2,1,0:T(8,128)(2,1)S(1)}, bf16[8,256,768]{2,1,0:T(8,128)(2,1)}) custom-call(f32[8,128]{1,0:T(8,128)S(1)} %get-tuple-element.21.total, bf16[512,2048]{1,0:T(8,128)(2,1)} %get-tuple-element.24.tok_in, bf16[512,2048]{1,0:T(8,128)(2,1)} %get-tuple-element.25.grad_in, ...), custom_call_target="tpu_custom_call" | custom-call | tf_op jit(solution)/shard_map/compute/pallas_call | solution.py:362
  123.7 38.3 %all_to_all.26.got = bf16[4,8,64,768]{3,2,1,0:T(8,128)(2,1)S(1)} all-to-all(bf16[4,8,64,768]{3,2,1,0:T(8,128)(2,1)S(1)} %get-tuple-element.27), channel_id=1, replica_groups=mesh['y'=8,'x'=4,'z'=8,'c'=2] {'x'}, dimensions={0} | all-to-all | bytes 6291456 | tf_op jit(solution)/shard_map/all_to_all | solution.py:273
  161.9 1.3 add_x.1
  163.2 5.8 %all-to-all-start.4 = ((bf16[8,64,768]{2,1,0:T(8,128)(2,1)}), bf16[8,64,768]{2,1,0:T(8,128)(2,1)S(1)}, u32[]{:S(2)}, u32[]{:S(2)}) async-start(bf16[8,64,768]{2,1,0:T(8,128)(2,1)} %add_x.1), calls=%async_computation.4 | async-start | bytes 1572864 | tf_op jit(solution)/shard_map/all_to_all | solution.py:273
  169.1 1.0 copy-done
  170.7 2.5 %collective-permute-start.9 = (bf16[64,768]{1,0:T(8,128)(2,1)S(1)}, bf16[64,768]{1,0:T(8,128)(2,1)S(1)}, u32[]{:S(2)}, u32[]{:S(2)}) collective-permute-start(bf16[64,768]{1,0:T(8,128)(2,1)S(1)} %get-tuple-element.30), channel_id=1, source_target_pairs={{0,16},{16,32},{32,48},{48,0},{1,17},{17,33},{33,49},{49,1},{2,18}... | collective-permute-start | bytes 294920 | tf_op jit(solution)/shard_map/ppermute | solution.py:412
  173.2 4.4 %collective-permute-start.10 = (bf16[64,768]{1,0:T(8,128)(2,1)S(1)}, bf16[64,768]{1,0:T(8,128)(2,1)S(1)}, u32[]{:S(2)}, u32[]{:S(2)}) collective-permute-start(bf16[64,768]{1,0:T(8,128)(2,1)S(1)} %get-tuple-element.31), channel_id=1, source_target_pairs={{0,32},{16,48},{32,0},{48,16},{1,33},{17,49},{33,1},{49,17},{2,34}... | collective-permute-start | bytes 294920 | tf_op jit(solution)/shard_map/ppermute | solution.py:412
  177.5 3.0 %collective-permute-start.11 = (bf16[64,768]{1,0:T(8,128)(2,1)S(1)}, bf16[64,768]{1,0:T(8,128)(2,1)S(1)}, u32[]{:S(2)}, u32[]{:S(2)}) collective-permute-start(bf16[64,768]{1,0:T(8,128)(2,1)S(1)} %get-tuple-element.32), channel_id=1, source_target_pairs={{0,48},{16,0},{32,16},{48,32},{1,49},{17,1},{33,17},{49,33},{2,50}... | collective-permute-start | bytes 294920 | tf_op jit(solution)/shard_map/ppermute | solution.py:412
  180.5 10.6 %all-to-all-done.4.from_y = bf16[8,64,768]{2,1,0:T(8,128)(2,1)S(1)} async-done(((bf16[8,64,768]{2,1,0:T(8,128)(2,1)}), bf16[8,64,768]{2,1,0:T(8,128)(2,1)S(1)}, u32[]{:S(2)}, u32[]{:S(2)}) %all-to-all-start.4) | async-done | bytes 786464 | tf_op jit(solution)/shard_map/all_to_all | solution.py:273
  (31 shorter events, 3.8 us)
Async XLA Ops:
  7.2 105.5 %all-gather.2.cloned.1.call-start = ((), (), s32[]{:S(2)}) async-start(), calls=%async_computation.6 | async-start | bytes 6488064 | tf_op jit(solution)/shard_map/all_gather | solution.py:293
  9.6 0.9 copy-start.1
  10.5 0.9 copy-start.2
  11.4 0.7 copy-start.3
  12.1 0.7 copy-start.6
  15.7 64.5 %copy-start.5 = (s32[16,3]{0,1:T(4,128)S(1)}, s32[16,3]{0,1:T(4,128)}, u32[]{:S(2)}) copy-start(s32[16,3]{0,1:T(4,128)} %param.11) | copy-start | bytes 580
  15.7 17.5 %all-to-all-start = ((bf16[4,528,128]{2,1,0:T(8,128)(2,1)}), bf16[4,528,128]{2,1,0:T(8,128)(2,1)S(1)}, u32[]{:S(2)}, u32[]{:S(2)}) async-start(bf16[4,528,128]{2,1,0:T(8,128)(2,1)} %get-tuple-element.20), calls=%async_computation | async-start | bytes 1081344 | tf_op jit(solution)/shard_map/all_to_all | solution.py:273
  20.7 30.7 %collective-permute-start.4 = (bf16[1024,128]{1,0:T(8,128)(2,1)S(1)}, bf16[1024,128]{1,0:T(8,128)(2,1)S(1)}, u32[]{:S(2)}, u32[]{:S(2)}) collective-permute-start(bf16[1024,128]{1,0:T(8,128)(2,1)S(1)} %get-tuple-element.22.refs_0_), channel_id=1, source_target_pairs={{0,12},{2,14},{4,0},{6,2},{8,4},{10,6},{12,8},{14,10},{1,13},{3,15... | collective-permute-start | bytes 786440 | tf_op jit(solution)/shard_map/ppermute | solution.py:281
  31.3 24.7 %collective-permute-start.1 = (bf16[1024,128]{1,0:T(8,128)(2,1)S(1)}, bf16[1024,128]{1,0:T(8,128)(2,1)S(1)}, u32[]{:S(2)}, u32[]{:S(2)}) collective-permute-start(bf16[1024,128]{1,0:T(8,128)(2,1)S(1)} %get-tuple-element.22.refs_0_), channel_id=1, source_target_pairs={{0,4},{2,6},{4,8},{6,10},{8,12},{10,14},{12,0},{14,2},{1,5},{3,7},... | collective-permute-start | bytes 786440 | tf_op jit(solution)/shard_map/ppermute | solution.py:281
  33.3 0.7 copy-start.4
  35.7 44.5 %all-to-all-start.1 = ((bf16[8,272,128]{2,1,0:T(8,128)(2,1)}), bf16[8,272,128]{2,1,0:T(8,128)(2,1)S(1)}, u32[]{:S(2)}, u32[]{:S(2)}) async-start(bf16[8,272,128]{2,1,0:T(8,128)(2,1)} %pack_y.1), calls=%async_computation.1 | async-start | bytes 1114112 | tf_op jit(solution)/shard_map/all_to_all | solution.py:273
  42.6 126.5 %reduce-scatter.2.cloned.1.call-start = ((), (), s32[]{:S(2)}) async-start(), calls=%async_computation.7 | async-start | bytes 3538944 | tf_op jit(solution)/shard_map/reduce_scatter | solution.py:391
  42.6 17.3 %collective-permute-start.6 = (bf16[1024,128]{1,0:T(8,128)(2,1)S(1)}, bf16[1024,128]{1,0:T(8,128)(2,1)S(1)}, u32[]{:S(2)}, u32[]{:S(2)}) collective-permute-start(bf16[1024,128]{1,0:T(8,128)(2,1)S(1)} %get-tuple-element.22.refs_0_), channel_id=1, source_target_pairs={{0,14},{2,0},{4,2},{6,4},{8,6},{10,8},{12,10},{14,12},{1,15},{3,1}... | collective-permute-start | bytes 786440 | tf_op jit(solution)/shard_map/ppermute | solution.py:281
  49.5 10.4 %collective-permute-start = (bf16[1024,128]{1,0:T(8,128)(2,1)S(1)}, bf16[1024,128]{1,0:T(8,128)(2,1)S(1)}, u32[]{:S(2)}, u32[]{:S(2)}) collective-permute-start(bf16[1024,128]{1,0:T(8,128)(2,1)S(1)} %get-tuple-element.22.refs_0_), channel_id=1, source_target_pairs={{0,2},{2,4},{4,6},{6,8},{8,10},{10,12},{12,14},{14,0},{1,3},{3,5},... | collective-permute-start | bytes 786440 | tf_op jit(solution)/shard_map/ppermute | solution.py:281
  51.4 8.5 %collective-permute-start.5 = (bf16[1024,128]{1,0:T(8,128)(2,1)S(1)}, bf16[1024,128]{1,0:T(8,128)(2,1)S(1)}, u32[]{:S(2)}, u32[]{:S(2)}) collective-permute-start(bf16[1024,128]{1,0:T(8,128)(2,1)S(1)} %collective-permute-done.4.refs_6_), channel_id=1, source_target_pairs={{0,14},{2,0},{4,2},{6,4},{8,6},{10,8},{12,10},{14,12},{1,15},{3,1}... | collective-permute-start | bytes 786440 | tf_op jit(solution)/shard_map/ppermute | solution.py:281
  56.0 13.3 %collective-permute-start.3 = (bf16[1024,128]{1,0:T(8,128)(2,1)S(1)}, bf16[1024,128]{1,0:T(8,128)(2,1)S(1)}, u32[]{:S(2)}, u32[]{:S(2)}) collective-permute-start(bf16[1024,128]{1,0:T(8,128)(2,1)S(1)} %collective-permute-done.1.refs_2_), channel_id=1, source_target_pairs={{0,4},{2,6},{4,8},{6,10},{8,12},{10,14},{12,0},{14,2},{1,5},{3,7},... | collective-permute-start | bytes 786440 | tf_op jit(solution)/shard_map/ppermute | solution.py:281
  57.9 17.4 %collective-permute-start.2 = (bf16[1024,128]{1,0:T(8,128)(2,1)S(1)}, bf16[1024,128]{1,0:T(8,128)(2,1)S(1)}, u32[]{:S(2)}, u32[]{:S(2)}) collective-permute-start(bf16[1024,128]{1,0:T(8,128)(2,1)S(1)} %collective-permute-done.1.refs_2_), channel_id=1, source_target_pairs={{0,2},{2,4},{4,6},{6,8},{8,10},{10,12},{12,14},{14,0},{1,3},{3,5},... | collective-permute-start | bytes 786440 | tf_op jit(solution)/shard_map/ppermute | solution.py:281
  75.5 28.4 %collective-permute-start.7 = (bf16[8,1024,128]{2,1,0:T(8,128)(2,1)S(1)}, bf16[8,1024,128]{2,1,0:T(8,128)(2,1)}, u32[]{:S(2)}, u32[]{:S(2)}) collective-permute-start(bf16[8,1024,128]{2,1,0:T(8,128)(2,1)S(1)} %gather_up.1.mine), channel_id=1, source_target_pairs={{0,1},{1,0},{2,3},{3,2},{4,5},{5,4},{6,7},{7,6},{8,9},{9,8},{10,11... | collective-permute-start | bytes 6291464 | tf_op jit(solution)/shard_map/ppermute | solution.py:277
  101.5 3.9 %collective-permute-start.8 = (bf16[8,256,128]{2,1,0:T(8,128)(2,1)S(1)}, bf16[8,256,128]{2,1,0:T(8,128)(2,1)S(1)}, u32[]{:S(2)}, u32[]{:S(2)}) collective-permute-start(bf16[8,256,128]{2,1,0:T(8,128)(2,1)S(1)} %all_to_all.25.late), channel_id=1, source_target_pairs={{0,1},{1,0},{2,3},{3,2},{4,5},{5,4},{6,7},{7,6},{8,9},{9,8},{10,11... | collective-permute-start | bytes 1572872 | tf_op jit(solution)/shard_map/ppermute | solution.py:277
  163.2 27.9 %all-to-all-start.4 = ((bf16[8,64,768]{2,1,0:T(8,128)(2,1)}), bf16[8,64,768]{2,1,0:T(8,128)(2,1)S(1)}, u32[]{:S(2)}, u32[]{:S(2)}) async-start(bf16[8,64,768]{2,1,0:T(8,128)(2,1)} %add_x.1), calls=%async_computation.4 | async-start | bytes 1572864 | tf_op jit(solution)/shard_map/all_to_all | solution.py:273
  169.1 1.0 copy-start
  170.7 20.4 %collective-permute-start.9 = (bf16[64,768]{1,0:T(8,128)(2,1)S(1)}, bf16[64,768]{1,0:T(8,128)(2,1)S(1)}, u32[]{:S(2)}, u32[]{:S(2)}) collective-permute-start(bf16[64,768]{1,0:T(8,128)(2,1)S(1)} %get-tuple-element.30), channel_id=1, source_target_pairs={{0,16},{16,32},{32,48},{48,0},{1,17},{17,33},{33,49},{49,1},{2,18}... | collective-permute-start | bytes 294920 | tf_op jit(solution)/shard_map/ppermute | solution.py:412
  173.2 17.9 %collective-permute-start.10 = (bf16[64,768]{1,0:T(8,128)(2,1)S(1)}, bf16[64,768]{1,0:T(8,128)(2,1)S(1)}, u32[]{:S(2)}, u32[]{:S(2)}) collective-permute-start(bf16[64,768]{1,0:T(8,128)(2,1)S(1)} %get-tuple-element.31), channel_id=1, source_target_pairs={{0,32},{16,48},{32,0},{48,16},{1,33},{17,49},{33,1},{49,17},{2,34}... | collective-permute-start | bytes 294920 | tf_op jit(solution)/shard_map/ppermute | solution.py:412
  177.5 13.6 %collective-permute-start.11 = (bf16[64,768]{1,0:T(8,128)(2,1)S(1)}, bf16[64,768]{1,0:T(8,128)(2,1)S(1)}, u32[]{:S(2)}, u32[]{:S(2)}) collective-permute-start(bf16[64,768]{1,0:T(8,128)(2,1)S(1)} %get-tuple-element.32), channel_id=1, source_target_pairs={{0,48},{16,0},{32,16},{48,32},{1,49},{17,1},{33,17},{49,33},{2,50}... | collective-permute-start | bytes 294920 | tf_op jit(solution)/shard_map/ppermute | solution.py:412
Sparse Core Ops, SparseCore 0:
  11.7 100.9 all-gather.1
  123.8 44.6 reduce-scatter.1

commit v2 on v1

--- a/solution.py
+++ b/solution.py
@@ -31,6 +31,18 @@
 
 def move_count(moves):
     return moves.shape[1]
+
+
+def stack_x(pos, *refs):
+    pieces, out, sems = refs[:NX], refs[NX], refs[NX + 1]
+    sends = [
+        pltpu.make_async_copy(piece, out.at[(pos[1] - k + NX) % NX], sems.at[k])
+        for k, piece in enumerate(pieces)
+    ]
+    for send in sends:
+        send.start()
+    for send in sends:
+        send.wait()
 
 
 def pack_x(pos, moves, seg, tok, grad, box, work, masked):
@@ -277,6 +289,10 @@
     return lax.ppermute(value, "c", [(0, 1), (1, 0)])
 
 
+def along_x(value, by):
+    return lax.ppermute(value, "x", [(i, (i + by) % NX) for i in range(NX)])
+
+
 def along_z(value, by):
     return lax.ppermute(value, "z", [(i, (i + by) % NZ) for i in range(NZ)])
 
@@ -290,11 +306,21 @@
     per, hid = gate_weight.shape
     span = WORK * BLOCK
     model = 2 * NZ * feat
-    weights = lax.all_gather(
-        jnp.concatenate([gate_weight, up_weight, down_weight], axis=1), ROW, axis=0, tiled=True
-    )
+    hbm = pl.BlockSpec(memory_space=pltpu.HBM)
     pos = jnp.stack([lax.axis_index("y"), lax.axis_index("x"), counts[0], lax.axis_index("c"), lax.axis_index("z")])
     moves = block_moves.T
+    joined = jnp.concatenate([gate_weight, up_weight, down_weight], axis=1)
+    shifted = [along_x(joined, k) for k in range(1, NX)]
+    stacked = pl.pallas_call(
+        stack_x,
+        out_shape=pltpu.HBM((NX, per, 3 * hid), bf),
+        in_specs=[smem()] + [pl.BlockSpec(memory_space=pl.ANY)] * NX,
+        out_specs=hbm,
+        scratch_shapes=[pltpu.SemaphoreType.DMA((NX,))],
+        compiler_params=params(8),
+        name="stack_x",
+    )(pos, joined, *shifted)
+    weights = lax.all_gather(stacked.reshape(NX * per, 3 * hid), "y", axis=0, tiled=True)
     box, work = pl.pallas_call(
         pack_x,
         out_shape=(
@@ -343,7 +369,6 @@
         name="gather_up",
     )(*pieces)
     other = swap(mine)
-    hbm = pl.BlockSpec(memory_space=pltpu.HBM)
     tok, grad = pl.pallas_call(
         lay_out,
         out_shape=(pltpu.HBM((span, model), bf), pltpu.HBM((span, model), bf)),
@@ -409,7 +434,7 @@
         name="turn",
     )(pos, part_y.reshape(NX, per, wide_y))
     from_x = [turned[0]] + [
-        lax.ppermute(turned[k], "x", [(i, (i + k) % NX) for i in range(NX)]) for k in range(1, NX)
+        along_x(turned[k], k) for k in range(1, NX)
     ]
     gate_grad, up_grad, down_grad = pl.pallas_call(
         finish,

time: 200 us -> 219 us (1.095)
  starting transfers between devices: 64.4 us -> 76 us
  waiting for transfers between devices: 29.7 us -> 33.9 us
    ppermute x3 -> x6, starting transfers between devices: 9.84 us -> 18.7 us  [along_x(): return lax.ppermute(value, 'x', [(i, (i + by) % NX) for i in range(NX)])]
    ppermute x3 -> x6, waiting for transfers between devices: 0.01 us -> 4.87 us  [along_x(): return lax.ppermute(value, 'x', [(i, (i + by) % NX) for i in range(NX)])]
    ppermute x7, starting transfers between devices: 29.8 us -> 32.6 us  [along_z(): return lax.ppermute(value, 'z', [(i, (i + by) % NZ) for i in range(NZ)])]
  transfers between devices with their start and end apart: 17 -> 20, of which waited for: 5 -> 6; matrix products, arithmetic and copies ran while one was open for 0% -> 0% of each run, Pallas kernels for 6% -> 6%
where the time goes in v2:
time: 219 us; the launch traced here: 218 us
  starting transfers between devices  76 us (35%)
  blocking collectives  59.9 us (27%)
  waiting for transfers between devices  33.9 us (15%)
  Pallas kernels  25.8 us (12%)
  between operations  15 us (7%)
  local copies, waits for them, and re-layouts  6.83 us (3%)
    all_to_all x2, blocking collectives, a2a(): return lax.all_to_all(value, axis, split_axis=0, concat_axis=0, tiled=True)  59.9 us
    ppermute x7, starting transfers between devices, along_z(): return lax.ppermute(value, 'z', [(i, (i + by) % NZ) for i in range(NZ)])  32.6 us
    ppermute x6, starting transfers between devices, along_x(): return lax.ppermute(value, 'x', [(i, (i + by) % NX) for i in range(NX)])  18.7 us
    all_to_all x3, starting transfers between devices, a2a(): return lax.all_to_all(value, axis, split_axis=0, concat_axis=0, tiled=True)  17.7 us
    ppermute x7, waiting for transfers between devices, along_z(): return lax.ppermute(value, 'z', [(i, (i + by) % NZ) for i in range(NZ)])  15.5 us
    all_to_all x3, waiting for transfers between devices, a2a(): return lax.all_to_all(value, axis, split_axis=0, concat_axis=0, tiled=True)  11.9 us
    pallas_call x1, Pallas kernels, step(): pl.pallas_call(compute, out_shape=(pltpu.HBM((span, hid), bf), pltpu.VMEM...  10.9 us
    ppermute x2, starting transfers between devices, swap(): return lax.ppermute(value, 'c', [(0, 1), (1, 0)])  6.98 us
  transfers between devices with their start and end apart: 20, of which 6 were waited for; matrix products, arithmetic and copies ran while one was open for 0% of the time, Pallas kernels for 6%

profile of v2, /device:TPU:1, one launch (start us, length us, event | category | flops | bytes accessed | tf_op | source)
XLA Modules:
  0.0 217.5 jit_solution(9381430170429578446)
XLA Ops:
  9.8 5.2 %collective-permute-start.11 = (bf16[64,1536]{1,0:T(8,128)(2,1)S(1)}, bf16[64,1536]{1,0:T(8,128)(2,1)S(1)}, u32[]{:S(2)}, u32[]{:S(2)}) collective-permute-start(bf16[64,1536]{1,0:T(8,128)(2,1)S(1)} %constant_dynamic-update-slice_fusion.refs_0_), channel_id=1, source_target_pairs={{0,48},{16,0},{32,16},{48,32},{1,49},{17,1},{33,17},{49,33},{2,50}... | collective-permute-start | bytes 589832 | tf_op jit(solution)/shard_map/ppermute | solution.py:293
  15.0 2.4 %collective-permute-start.10 = (bf16[64,1536]{1,0:T(8,128)(2,1)S(1)}, bf16[64,1536]{1,0:T(8,128)(2,1)S(1)}, u32[]{:S(2)}, u32[]{:S(2)}) collective-permute-start(bf16[64,1536]{1,0:T(8,128)(2,1)S(1)} %constant_dynamic-update-slice_fusion.refs_0_), channel_id=1, source_target_pairs={{0,32},{16,48},{32,0},{48,16},{1,33},{17,49},{33,1},{49,17},{2,34}... | collective-permute-start | bytes 589832 | tf_op jit(solution)/shard_map/ppermute | solution.py:293
  17.4 2.5 %collective-permute-start.9 = (bf16[64,1536]{1,0:T(8,128)(2,1)S(1)}, bf16[64,1536]{1,0:T(8,128)(2,1)S(1)}, u32[]{:S(2)}, u32[]{:S(2)}) collective-permute-start(bf16[64,1536]{1,0:T(8,128)(2,1)S(1)} %constant_dynamic-update-slice_fusion.refs_0_), channel_id=1, source_target_pairs={{0,16},{16,32},{32,48},{48,0},{1,17},{17,33},{33,49},{49,1},{2,18}... | collective-permute-start | bytes 589832 | tf_op jit(solution)/shard_map/ppermute | solution.py:293
  20.7 2.2 %collective-permute-done.10.refs_2_ = bf16[64,1536]{1,0:T(8,128)(2,1)S(1)} collective-permute-done((bf16[64,1536]{1,0:T(8,128)(2,1)S(1)}, bf16[64,1536]{1,0:T(8,128)(2,1)S(1)}, u32[]{:S(2)}, u32[]{:S(2)}) %collective-permute-start.10) | collective-permute-done | bytes 196640 | tf_op jit(solution)/shard_map/ppermute | solution.py:293
  22.9 2.6 %collective-permute-done.9.refs_1_ = bf16[64,1536]{1,0:T(8,128)(2,1)S(1)} collective-permute-done((bf16[64,1536]{1,0:T(8,128)(2,1)S(1)}, bf16[64,1536]{1,0:T(8,128)(2,1)S(1)}, u32[]{:S(2)}, u32[]{:S(2)}) %collective-permute-start.9) | collective-permute-done | bytes 196640 | tf_op jit(solution)/shard_map/ppermute | solution.py:293
  25.5 1.5 stack_x.1
  30.3 2.9 %pack_x.1 = (bf16[4,528,128]{2,1,0:T(8,128)(2,1)}, bf16[1024,128]{1,0:T(8,128)(2,1)S(1)}) custom-call(s32[5]{0:T(128)S(1)} %stack.19.pos, s32[3,16]{1,0:T(4,128)S(1)} %bitcast.10, s32[6,128]{1,0:T(8,128)S(1)} %bitcast.14, bf16[768,128]{1,0:T(8,128)(2,1)S(1)} %copy-done.1, bf16[768,128]{1,0:T(8,128)(2,1)S(1)} %copy-done.2), custom_call_target="tpu_custom_call" | custom-call | tf_op jit(solution)/shard_map/pack_x/pallas_call | solution.py:324
  33.2 4.1 %all-to-all-start = ((bf16[4,528,128]{2,1,0:T(8,128)(2,1)}), bf16[4,528,128]{2,1,0:T(8,128)(2,1)S(1)}, u32[]{:S(2)}, u32[]{:S(2)}) async-start(bf16[4,528,128]{2,1,0:T(8,128)(2,1)} %get-tuple-element.20), calls=%async_computation | async-start | bytes 1081344 | tf_op jit(solution)/shard_map/all_to_all | solution.py:285
  37.3 13.5 %collective-permute-start.4 = (bf16[1024,128]{1,0:T(8,128)(2,1)S(1)}, bf16[1024,128]{1,0:T(8,128)(2,1)S(1)}, u32[]{:S(2)}, u32[]{:S(2)}) collective-permute-start(bf16[1024,128]{1,0:T(8,128)(2,1)S(1)} %get-tuple-element.22.refs_0_), channel_id=1, source_target_pairs={{0,12},{2,14},{4,0},{6,2},{8,4},{10,6},{12,8},{14,10},{1,13},{3,15... | collective-permute-start | bytes 786440 | tf_op jit(solution)/shard_map/ppermute | solution.py:297
  50.8 1.9 collective-permute-start.1
  52.8 1.7 pack_y.1
  54.5 6.8 %all-to-all-start.1 = ((bf16[8,272,128]{2,1,0:T(8,128)(2,1)}), bf16[8,272,128]{2,1,0:T(8,128)(2,1)S(1)}, u32[]{:S(2)}, u32[]{:S(2)}) async-start(bf16[8,272,128]{2,1,0:T(8,128)(2,1)} %pack_y.1), calls=%async_computation.1 | async-start | bytes 1114112 | tf_op jit(solution)/shard_map/all_to_all | solution.py:285
  61.3 6.9 %collective-permute-start.6 = (bf16[1024,128]{1,0:T(8,128)(2,1)S(1)}, bf16[1024,128]{1,0:T(8,128)(2,1)S(1)}, u32[]{:S(2)}, u32[]{:S(2)}) collective-permute-start(bf16[1024,128]{1,0:T(8,128)(2,1)S(1)} %get-tuple-element.22.refs_0_), channel_id=1, source_target_pairs={{0,14},{2,0},{4,2},{6,4},{8,6},{10,8},{12,10},{14,12},{1,15},{3,1}... | collective-permute-start | bytes 786440 | tf_op jit(solution)/shard_map/ppermute | solution.py:297
  68.2 1.9 collective-permute-start
  70.1 4.6 %collective-permute-start.5 = (bf16[1024,128]{1,0:T(8,128)(2,1)S(1)}, bf16[1024,128]{1,0:T(8,128)(2,1)S(1)}, u32[]{:S(2)}, u32[]{:S(2)}) collective-permute-start(bf16[1024,128]{1,0:T(8,128)(2,1)S(1)} %collective-permute-done.4.refs_6_), channel_id=1, source_target_pairs={{0,14},{2,0},{4,2},{6,4},{8,6},{10,8},{12,10},{14,12},{1,15},{3,1}... | collective-permute-start | bytes 786440 | tf_op jit(solution)/shard_map/ppermute | solution.py:297
  74.7 1.9 collective-permute-start.3
  76.7 1.9 collective-permute-start.2
  78.6 9.4 %collective-permute-done.3.refs_4_ = bf16[1024,128]{1,0:T(8,128)(2,1)S(1)} collective-permute-done((bf16[1024,128]{1,0:T(8,128)(2,1)S(1)}, bf16[1024,128]{1,0:T(8,128)(2,1)S(1)}, u32[]{:S(2)}, u32[]{:S(2)}) %collective-permute-start.3) | collective-permute-done | bytes 262176 | tf_op jit(solution)/shard_map/ppermute | solution.py:297
  88.1 6.1 %collective-permute-done.2.refs_3_ = bf16[1024,128]{1,0:T(8,128)(2,1)S(1)} collective-permute-done((bf16[1024,128]{1,0:T(8,128)(2,1)S(1)}, bf16[1024,128]{1,0:T(8,128)(2,1)S(1)}, u32[]{:S(2)}, u32[]{:S(2)}) %collective-permute-start.2) | collective-permute-done | bytes 262176 | tf_op jit(solution)/shard_map/ppermute | solution.py:297
  94.3 4.6 %collective-permute-start.7 = (bf16[8,1024,128]{2,1,0:T(8,128)(2,1)S(1)}, bf16[8,1024,128]{2,1,0:T(8,128)(2,1)}, u32[]{:S(2)}, u32[]{:S(2)}) collective-permute-start(bf16[8,1024,128]{2,1,0:T(8,128)(2,1)S(1)} %gather_up.1.mine), channel_id=1, source_target_pairs={{0,1},{1,0},{2,3},{3,2},{4,5},{5,4},{6,7},{7,6},{8,9},{9,8},{10,11... | collective-permute-start | bytes 6291464 | tf_op jit(solution)/shard_map/ppermute | solution.py:289
  99.8 20.4 %all_to_all.25.late = bf16[8,256,128]{2,1,0:T(8,128)(2,1)S(1)} all-to-all(bf16[8,256,128]{2,1,0:T(8,128)(2,1)S(1)} %get-tuple-element.23), channel_id=1, replica_groups=mesh['y'=8,'x'=4,'z'=8,'c'=2] {'z'}, dimensions={0} | all-to-all | bytes 1048576 | tf_op jit(solution)/shard_map/all_to_all | solution.py:285
  120.2 2.3 %collective-permute-start.8 = (bf16[8,256,128]{2,1,0:T(8,128)(2,1)S(1)}, bf16[8,256,128]{2,1,0:T(8,128)(2,1)S(1)}, u32[]{:S(2)}, u32[]{:S(2)}) collective-permute-start(bf16[8,256,128]{2,1,0:T(8,128)(2,1)S(1)} %all_to_all.25.late), channel_id=1, source_target_pairs={{0,1},{1,0},{2,3},{3,2},{4,5},{5,4},{6,7},{7,6},{8,9},{9,8},{10,11... | collective-permute-start | bytes 1572872 | tf_op jit(solution)/shard_map/ppermute | solution.py:289
  122.5 1.5 collective-permute-done.8.late_other
  124.1 5.1 %lay_out.1 = (bf16[512,2048]{1,0:T(8,128)(2,1)}, bf16[512,2048]{1,0:T(8,128)(2,1)}) custom-call(s32[5]{0:T(128)S(1)} %stack.19.pos, s32[3,16]{1,0:T(4,128)S(1)} %bitcast.13, bf16[8,1024,128]{2,1,0:T(8,128)(2,1)S(1)} %gather_up.1.mine, bf16[8,1024,128]{2,1,0:T(8,128)(2,1)} %collective-permute-done.7.other, bf16[8,256,128]{2,1,0:T(8,128)(2,1)S(1)} %all_to_all.25.late, ...), custom_call_target="tpu_custom_call" | custom-call | tf_op jit(solution)/shard_map/lay_out/pallas_call | solution.py:372
  129.2 10.9 %compute.1 = (bf16[512,512]{1,0:T(8,128)(2,1)}, bf16[4,8,64,768]{3,2,1,0:T(8,128)(2,1)S(1)}, bf16[8,256,768]{2,1,0:T(8,128)(2,1)}) custom-call(f32[8,128]{1,0:T(8,128)S(1)} %get-tuple-element.21.total, bf16[512,2048]{1,0:T(8,128)(2,1)} %get-tuple-element.24.tok_in, bf16[512,2048]{1,0:T(8,128)(2,1)} %get-tuple-element.25.grad_in, ...), custom_call_target="tpu_custom_call" | custom-call | tf_op jit(solution)/shard_map/compute/pallas_call | solution.py:387
  140.2 39.5 %all_to_all.26.got = bf16[4,8,64,768]{3,2,1,0:T(8,128)(2,1)S(1)} all-to-all(bf16[4,8,64,768]{3,2,1,0:T(8,128)(2,1)S(1)} %get-tuple-element.27), channel_id=1, replica_groups=mesh['y'=8,'x'=4,'z'=8,'c'=2] {'x'}, dimensions={0} | all-to-all | bytes 6291456 | tf_op jit(solution)/shard_map/all_to_all | solution.py:285
  179.7 1.3 add_x.1
  181.0 6.8 %all-to-all-start.4 = ((bf16[8,64,768]{2,1,0:T(8,128)(2,1)}), bf16[8,64,768]{2,1,0:T(8,128)(2,1)S(1)}, u32[]{:S(2)}, u32[]{:S(2)}) async-start(bf16[8,64,768]{2,1,0:T(8,128)(2,1)} %add_x.1), calls=%async_computation.4 | async-start | bytes 1572864 | tf_op jit(solution)/shard_map/all_to_all | solution.py:285
  189.3 2.3 %collective-permute-start.12 = (bf16[64,768]{1,0:T(8,128)(2,1)S(1)}, bf16[64,768]{1,0:T(8,128)(2,1)S(1)}, u32[]{:S(2)}, u32[]{:S(2)}) collective-permute-start(bf16[64,768]{1,0:T(8,128)(2,1)S(1)} %get-tuple-element.30), channel_id=1, source_target_pairs={{0,16},{16,32},{32,48},{48,0},{1,17},{17,33},{33,49},{49,1},{2,18}... | collective-permute-start | bytes 294920 | tf_op jit(solution)/shard_map/ppermute | solution.py:293
  191.7 3.6 %collective-permute-start.13 = (bf16[64,768]{1,0:T(8,128)(2,1)S(1)}, bf16[64,768]{1,0:T(8,128)(2,1)S(1)}, u32[]{:S(2)}, u32[]{:S(2)}) collective-permute-start(bf16[64,768]{1,0:T(8,128)(2,1)S(1)} %get-tuple-element.31), channel_id=1, source_target_pairs={{0,32},{16,48},{32,0},{48,16},{1,33},{17,49},{33,1},{49,17},{2,34}... | collective-permute-start | bytes 294920 | tf_op jit(solution)/shard_map/ppermute | solution.py:293
  195.2 2.7 %collective-permute-start.14 = (bf16[64,768]{1,0:T(8,128)(2,1)S(1)}, bf16[64,768]{1,0:T(8,128)(2,1)S(1)}, u32[]{:S(2)}, u32[]{:S(2)}) collective-permute-start(bf16[64,768]{1,0:T(8,128)(2,1)S(1)} %get-tuple-element.32), channel_id=1, source_target_pairs={{0,48},{16,0},{32,16},{48,32},{1,49},{17,1},{33,17},{49,33},{2,50}... | collective-permute-start | bytes 294920 | tf_op jit(solution)/shard_map/ppermute | solution.py:293
  197.9 11.9 %all-to-all-done.4.from_y = bf16[8,64,768]{2,1,0:T(8,128)(2,1)S(1)} async-done(((bf16[8,64,768]{2,1,0:T(8,128)(2,1)}), bf16[8,64,768]{2,1,0:T(8,128)(2,1)S(1)}, u32[]{:S(2)}, u32[]{:S(2)}) %all-to-all-start.4) | async-done | bytes 786464 | tf_op jit(solution)/shard_map/all_to_all | solution.py:285
  (38 shorter events, 9.3 us)
Async XLA Ops:
  7.2 45.6 %copy-start.4 = (s32[16,3]{0,1:T(4,128)S(1)}, s32[16,3]{0,1:T(4,128)}, u32[]{:S(2)}) copy-start(s32[16,3]{0,1:T(4,128)} %param.11) | copy-start | bytes 580
  7.2 122.0 %all-gather.2.cloned.1.call-start = ((), (), s32[]{:S(2)}) async-start(), calls=%async_computation.6 | async-start | bytes 7077888 | tf_op jit(solution)/shard_map/all_gather | solution.py:323
  9.8 10.9 %collective-permute-start.11 = (bf16[64,1536]{1,0:T(8,128)(2,1)S(1)}, bf16[64,1536]{1,0:T(8,128)(2,1)S(1)}, u32[]{:S(2)}, u32[]{:S(2)}) collective-permute-start(bf16[64,1536]{1,0:T(8,128)(2,1)S(1)} %constant_dynamic-update-slice_fusion.refs_0_), channel_id=1, source_target_pairs={{0,48},{16,0},{32,16},{48,32},{1,49},{17,1},{33,17},{49,33},{2,50}... | collective-permute-start | bytes 589832 | tf_op jit(solution)/shard_map/ppermute | solution.py:293
  15.0 7.9 %collective-permute-start.10 = (bf16[64,1536]{1,0:T(8,128)(2,1)S(1)}, bf16[64,1536]{1,0:T(8,128)(2,1)S(1)}, u32[]{:S(2)}, u32[]{:S(2)}) collective-permute-start(bf16[64,1536]{1,0:T(8,128)(2,1)S(1)} %constant_dynamic-update-slice_fusion.refs_0_), channel_id=1, source_target_pairs={{0,32},{16,48},{32,0},{48,16},{1,33},{17,49},{33,1},{49,17},{2,34}... | collective-permute-start | bytes 589832 | tf_op jit(solution)/shard_map/ppermute | solution.py:293
  17.4 8.1 %collective-permute-start.9 = (bf16[64,1536]{1,0:T(8,128)(2,1)S(1)}, bf16[64,1536]{1,0:T(8,128)(2,1)S(1)}, u32[]{:S(2)}, u32[]{:S(2)}) collective-permute-start(bf16[64,1536]{1,0:T(8,128)(2,1)S(1)} %constant_dynamic-update-slice_fusion.refs_0_), channel_id=1, source_target_pairs={{0,16},{16,32},{32,48},{48,0},{1,17},{17,33},{33,49},{49,1},{2,18}... | collective-permute-start | bytes 589832 | tf_op jit(solution)/shard_map/ppermute | solution.py:293
  27.1 0.9 copy-start.1
  28.0 0.9 copy-start.2
  28.9 0.7 copy-start.3
  29.6 0.7 copy-start.5
  33.2 19.5 %all-to-all-start = ((bf16[4,528,128]{2,1,0:T(8,128)(2,1)}), bf16[4,528,128]{2,1,0:T(8,128)(2,1)S(1)}, u32[]{:S(2)}, u32[]{:S(2)}) async-start(bf16[4,528,128]{2,1,0:T(8,128)(2,1)} %get-tuple-element.20), calls=%async_computation | async-start | bytes 1081344 | tf_op jit(solution)/shard_map/all_to_all | solution.py:285
  37.3 32.8 %collective-permute-start.4 = (bf16[1024,128]{1,0:T(8,128)(2,1)S(1)}, bf16[1024,128]{1,0:T(8,128)(2,1)S(1)}, u32[]{:S(2)}, u32[]{:S(2)}) collective-permute-start(bf16[1024,128]{1,0:T(8,128)(2,1)S(1)} %get-tuple-element.22.refs_0_), channel_id=1, source_target_pairs={{0,12},{2,14},{4,0},{6,2},{8,4},{10,6},{12,8},{14,10},{1,13},{3,15... | collective-permute-start | bytes 786440 | tf_op jit(solution)/shard_map/ppermute | solution.py:297
  50.8 23.9 %collective-permute-start.1 = (bf16[1024,128]{1,0:T(8,128)(2,1)S(1)}, bf16[1024,128]{1,0:T(8,128)(2,1)S(1)}, u32[]{:S(2)}, u32[]{:S(2)}) collective-permute-start(bf16[1024,128]{1,0:T(8,128)(2,1)S(1)} %get-tuple-element.22.refs_0_), channel_id=1, source_target_pairs={{0,4},{2,6},{4,8},{6,10},{8,12},{10,14},{12,0},{14,2},{1,5},{3,7},... | collective-permute-start | bytes 786440 | tf_op jit(solution)/shard_map/ppermute | solution.py:297
  54.5 44.4 %all-to-all-start.1 = ((bf16[8,272,128]{2,1,0:T(8,128)(2,1)}), bf16[8,272,128]{2,1,0:T(8,128)(2,1)S(1)}, u32[]{:S(2)}, u32[]{:S(2)}) async-start(bf16[8,272,128]{2,1,0:T(8,128)(2,1)} %pack_y.1), calls=%async_computation.1 | async-start | bytes 1114112 | tf_op jit(solution)/shard_map/all_to_all | solution.py:285
  61.3 126.4 %reduce-scatter.2.cloned.1.call-start = ((), (), s32[]{:S(2)}) async-start(), calls=%async_computation.7 | async-start | bytes 3538944 | tf_op jit(solution)/shard_map/reduce_scatter | solution.py:416
  61.3 17.3 %collective-permute-start.6 = (bf16[1024,128]{1,0:T(8,128)(2,1)S(1)}, bf16[1024,128]{1,0:T(8,128)(2,1)S(1)}, u32[]{:S(2)}, u32[]{:S(2)}) collective-permute-start(bf16[1024,128]{1,0:T(8,128)(2,1)S(1)} %get-tuple-element.22.refs_0_), channel_id=1, source_target_pairs={{0,14},{2,0},{4,2},{6,4},{8,6},{10,8},{12,10},{14,12},{1,15},{3,1}... | collective-permute-start | bytes 786440 | tf_op jit(solution)/shard_map/ppermute | solution.py:297
  68.2 10.4 %collective-permute-start = (bf16[1024,128]{1,0:T(8,128)(2,1)S(1)}, bf16[1024,128]{1,0:T(8,128)(2,1)S(1)}, u32[]{:S(2)}, u32[]{:S(2)}) collective-permute-start(bf16[1024,128]{1,0:T(8,128)(2,1)S(1)} %get-tuple-element.22.refs_0_), channel_id=1, source_target_pairs={{0,2},{2,4},{4,6},{6,8},{8,10},{10,12},{12,14},{14,0},{1,3},{3,5},... | collective-permute-start | bytes 786440 | tf_op jit(solution)/shard_map/ppermute | solution.py:297
  70.1 8.5 %collective-permute-start.5 = (bf16[1024,128]{1,0:T(8,128)(2,1)S(1)}, bf16[1024,128]{1,0:T(8,128)(2,1)S(1)}, u32[]{:S(2)}, u32[]{:S(2)}) collective-permute-start(bf16[1024,128]{1,0:T(8,128)(2,1)S(1)} %collective-permute-done.4.refs_6_), channel_id=1, source_target_pairs={{0,14},{2,0},{4,2},{6,4},{8,6},{10,8},{12,10},{14,12},{1,15},{3,1}... | collective-permute-start | bytes 786440 | tf_op jit(solution)/shard_map/ppermute | solution.py:297
  74.7 13.3 %collective-permute-start.3 = (bf16[1024,128]{1,0:T(8,128)(2,1)S(1)}, bf16[1024,128]{1,0:T(8,128)(2,1)S(1)}, u32[]{:S(2)}, u32[]{:S(2)}) collective-permute-start(bf16[1024,128]{1,0:T(8,128)(2,1)S(1)} %collective-permute-done.1.refs_2_), channel_id=1, source_target_pairs={{0,4},{2,6},{4,8},{6,10},{8,12},{10,14},{12,0},{14,2},{1,5},{3,7},... | collective-permute-start | bytes 786440 | tf_op jit(solution)/shard_map/ppermute | solution.py:297
  76.7 17.5 %collective-permute-start.2 = (bf16[1024,128]{1,0:T(8,128)(2,1)S(1)}, bf16[1024,128]{1,0:T(8,128)(2,1)S(1)}, u32[]{:S(2)}, u32[]{:S(2)}) collective-permute-start(bf16[1024,128]{1,0:T(8,128)(2,1)S(1)} %collective-permute-done.1.refs_2_), channel_id=1, source_target_pairs={{0,2},{2,4},{4,6},{6,8},{8,10},{10,12},{12,14},{14,0},{1,3},{3,5},... | collective-permute-start | bytes 786440 | tf_op jit(solution)/shard_map/ppermute | solution.py:297
  94.3 28.2 %collective-permute-start.7 = (bf16[8,1024,128]{2,1,0:T(8,128)(2,1)S(1)}, bf16[8,1024,128]{2,1,0:T(8,128)(2,1)}, u32[]{:S(2)}, u32[]{:S(2)}) collective-permute-start(bf16[8,1024,128]{2,1,0:T(8,128)(2,1)S(1)} %gather_up.1.mine), channel_id=1, source_target_pairs={{0,1},{1,0},{2,3},{3,2},{4,5},{5,4},{6,7},{7,6},{8,9},{9,8},{10,11... | collective-permute-start | bytes 6291464 | tf_op jit(solution)/shard_map/ppermute | solution.py:289
  120.2 3.9 %collective-permute-start.8 = (bf16[8,256,128]{2,1,0:T(8,128)(2,1)S(1)}, bf16[8,256,128]{2,1,0:T(8,128)(2,1)S(1)}, u32[]{:S(2)}, u32[]{:S(2)}) collective-permute-start(bf16[8,256,128]{2,1,0:T(8,128)(2,1)S(1)} %all_to_all.25.late), channel_id=1, source_target_pairs={{0,1},{1,0},{2,3},{3,2},{4,5},{5,4},{6,7},{7,6},{8,9},{9,8},{10,11... | collective-permute-start | bytes 1572872 | tf_op jit(solution)/shard_map/ppermute | solution.py:289
  181.0 28.9 %all-to-all-start.4 = ((bf16[8,64,768]{2,1,0:T(8,128)(2,1)}), bf16[8,64,768]{2,1,0:T(8,128)(2,1)S(1)}, u32[]{:S(2)}, u32[]{:S(2)}) async-start(bf16[8,64,768]{2,1,0:T(8,128)(2,1)} %add_x.1), calls=%async_computation.4 | async-start | bytes 1572864 | tf_op jit(solution)/shard_map/all_to_all | solution.py:285
  187.8 1.0 copy-start
  189.3 20.5 %collective-permute-start.12 = (bf16[64,768]{1,0:T(8,128)(2,1)S(1)}, bf16[64,768]{1,0:T(8,128)(2,1)S(1)}, u32[]{:S(2)}, u32[]{:S(2)}) collective-permute-start(bf16[64,768]{1,0:T(8,128)(2,1)S(1)} %get-tuple-element.30), channel_id=1, source_target_pairs={{0,16},{16,32},{32,48},{48,0},{1,17},{17,33},{33,49},{49,1},{2,18}... | collective-permute-start | bytes 294920 | tf_op jit(solution)/shard_map/ppermute | solution.py:293
  191.7 18.2 %collective-permute-start.13 = (bf16[64,768]{1,0:T(8,128)(2,1)S(1)}, bf16[64,768]{1,0:T(8,128)(2,1)S(1)}, u32[]{:S(2)}, u32[]{:S(2)}) collective-permute-start(bf16[64,768]{1,0:T(8,128)(2,1)S(1)} %get-tuple-element.31), channel_id=1, source_target_pairs={{0,32},{16,48},{32,0},{48,16},{1,33},{17,49},{33,1},{49,17},{2,34}... | collective-permute-start | bytes 294920 | tf_op jit(solution)/shard_map/ppermute | solution.py:293
  195.2 14.6 %collective-permute-start.14 = (bf16[64,768]{1,0:T(8,128)(2,1)S(1)}, bf16[64,768]{1,0:T(8,128)(2,1)S(1)}, u32[]{:S(2)}, u32[]{:S(2)}) collective-permute-start(bf16[64,768]{1,0:T(8,128)(2,1)S(1)} %get-tuple-element.32), channel_id=1, source_target_pairs={{0,48},{16,0},{32,16},{48,32},{1,49},{17,1},{33,17},{49,33},{2,50}... | collective-permute-start | bytes 294920 | tf_op jit(solution)/shard_map/ppermute | solution.py:293
Sparse Core Ops, SparseCore 0:
  27.2 94.6 all-gather.1
  140.3 40.8 reduce-scatter.1

commit v3 on v1

--- a/solution.py
+++ b/solution.py
@@ -189,24 +189,26 @@
     tile = width // 2
     per = by_x.shape[2]
     cut = by_x.shape[3] - width
-    fore = 2 * width
-    loads = (
-        pltpu.make_async_copy(tok_in, tok, in_sem.at[0]),
-        pltpu.make_async_copy(weights.at[:, :fore], held.at[:, :fore], in_sem.at[1]),
-        pltpu.make_async_copy(grad_in, grad, in_sem.at[2]),
-        pltpu.make_async_copy(weights.at[:, fore:], held.at[:, fore:], in_sem.at[3]),
-    )
-    for load in loads:
+    thirds = [slice(k * width, (k + 1) * width) for k in range(3)]
+    take_tok = pltpu.make_async_copy(tok_in, tok, in_sem.at[3])
+    take_grad = pltpu.make_async_copy(grad_in, grad, in_sem.at[4])
+    take = [
+        pltpu.make_async_copy(weights.at[:, cols], held.at[:, cols], in_sem.at[k])
+        for k, cols in enumerate(thirds)
+    ]
+    for load in (take_tok, take[0], take[1], take_grad, take[2]):
         load.start()
-    loads[0].wait()
-    loads[1].wait()
-    sums = jnp.dot(tok[...], held[:, :fore], preferred_element_type=jnp.float32)
-    loads[2].wait()
-    loads[3].wait()
+    take_tok.wait()
+    take[0].wait()
+    gate_all = jnp.dot(tok[...], held[:, thirds[0]], preferred_element_type=jnp.float32)
+    take[1].wait()
+    up_all = jnp.dot(tok[...], held[:, thirds[1]], preferred_element_type=jnp.float32)
+    take_grad.wait()
+    take[2].wait()
     for at in range(0, width, tile):
-        gate_sum = sums[:, at : at + tile]
-        up_sum = sums[:, width + at : width + at + tile]
-        down_w = held[:, fore + at : fore + at + tile]
+        gate_sum = gate_all[:, at : at + tile]
+        up_sum = up_all[:, at : at + tile]
+        down_w = held[:, 2 * width + at : 2 * width + at + tile]
         back_sum = jnp.dot(grad[...], down_w, preferred_element_type=jnp.float32)
         logistic = jax.nn.sigmoid(gate_sum)
         act = gate_sum * logistic
@@ -227,15 +229,18 @@
 
     stores = []
     for y in range(NY):
-        at = y * NX * per
-        both = term(tok[:, at : at + NX * per], back[...])
-        for x in range(NX):
-            by_x[x, y, :, :width] = both[x * per : (x + 1) * per, width:]
-            by_x[x, y, :, width:] = both[x * per : (x + 1) * per, :cut]
-        stage[y, :, : width - cut] = both[:, cut:width]
-        stage[y, :, width - cut :] = term(grad[:, at : at + NX * per], hid[...])
+        rows = slice(y * NX * per, (y + 1) * NX * per)
+        stage[y, :, : width - cut] = term(tok[:, rows], back[:, cut:width])
+        stage[y, :, width - cut :] = term(grad[:, rows], hid[...])
         stores.append(pltpu.make_async_copy(stage.at[y], by_y.at[y], out_sem.at[y]))
         stores[y].start()
+    for y in range(NY):
+        rows = slice(y * NX * per, (y + 1) * NX * per)
+        up = term(tok[:, rows], back[:, width:])
+        gate = term(tok[:, rows], back[:, :cut])
+        for x in range(NX):
+            by_x[x, y, :, :width] = up[x * per : (x + 1) * per]
+            by_x[x, y, :, width:] = gate[x * per : (x + 1) * per]
     for store in stores:
         store.wait()
     keep.wait()
@@ -375,7 +380,7 @@
             pltpu.VMEM((span, hid), bf),
             pltpu.VMEM((span, 2 * hid), bf),
             pltpu.VMEM((NY, NX * per, wide_y), bf),
-            pltpu.SemaphoreType.DMA((4,)),
+            pltpu.SemaphoreType.DMA((5,)),
             pltpu.SemaphoreType.DMA((NY,)),
             pltpu.SemaphoreType.DMA(()),
         ],

time: 200 us -> 199 us (level)
  no operation moved by 1% of the time
where the time goes in v3:
time: 199 us; the launch traced here: 198 us
  starting transfers between devices  64.4 us (32%)
  blocking collectives  58.7 us (29%)
  waiting for transfers between devices  29.8 us (15%)
  Pallas kernels  23.4 us (12%)
  between operations  14.9 us (7%)
  local copies, waits for them, and re-layouts  4.98 us (3%)
    all_to_all x2, blocking collectives, a2a(): return lax.all_to_all(value, axis, split_axis=0, concat_axis=0, tiled=True)  58.7 us
    ppermute x7, starting transfers between devices, along_z(): return lax.ppermute(value, 'z', [(i, (i + by) % NZ) for i in range(NZ)])  29.8 us
    all_to_all x3, starting transfers between devices, a2a(): return lax.all_to_all(value, axis, split_axis=0, concat_axis=0, tiled=True)  17.6 us
    ppermute x7, waiting for transfers between devices, along_z(): return lax.ppermute(value, 'z', [(i, (i + by) % NZ) for i in range(NZ)])  15.4 us
    all_to_all x3, waiting for transfers between devices, a2a(): return lax.all_to_all(value, axis, split_axis=0, concat_axis=0, tiled=True)  10.6 us
    pallas_call x1, Pallas kernels, step(): pl.pallas_call(compute, out_shape=(pltpu.HBM((span, hid), bf), pltpu.VMEM...  9.91 us
    ppermute x3, starting transfers between devices, step(): lax.ppermute(turned[k], 'x', [(i, (i + k) % NX) for i in range(NX)])  9.82 us
    ppermute x2, starting transfers between devices, swap(): return lax.ppermute(value, 'c', [(0, 1), (1, 0)])  7.09 us
  transfers between devices with their start and end apart: 17, of which 5 were waited for; matrix products, arithmetic and copies ran while one was open for 0% of the time, Pallas kernels for 6%

profile of v3, /device:TPU:1, one launch (start us, length us, event | category | flops | bytes accessed | tf_op | source)
XLA Modules:
  0.0 197.7 jit_solution(10462206712192154512)
XLA Ops:
  7.2 1.6 pad_maximum_fusion
  9.6 0.9 copy-done.1
  10.5 0.9 copy-done.2
  12.8 2.9 %pack_x.1 = (bf16[4,528,128]{2,1,0:T(8,128)(2,1)}, bf16[1024,128]{1,0:T(8,128)(2,1)S(1)}) custom-call(s32[5]{0:T(128)S(1)} %stack.19.pos, s32[3,16]{1,0:T(4,128)S(1)} %bitcast.9, s32[6,128]{1,0:T(8,128)S(1)} %bitcast.13, bf16[768,128]{1,0:T(8,128)(2,1)S(1)} %copy-done.1, bf16[768,128]{1,0:T(8,128)(2,1)S(1)} %copy-done.2), custom_call_target="tpu_custom_call" | custom-call | tf_op jit(solution)/shard_map/pack_x/pallas_call | solution.py:303
  15.7 4.9 %all-to-all-start = ((bf16[4,528,128]{2,1,0:T(8,128)(2,1)}), bf16[4,528,128]{2,1,0:T(8,128)(2,1)S(1)}, u32[]{:S(2)}, u32[]{:S(2)}) async-start(bf16[4,528,128]{2,1,0:T(8,128)(2,1)} %get-tuple-element.20), calls=%async_computation | async-start | bytes 1081344 | tf_op jit(solution)/shard_map/all_to_all | solution.py:278
  20.7 10.6 %collective-permute-start.4 = (bf16[1024,128]{1,0:T(8,128)(2,1)S(1)}, bf16[1024,128]{1,0:T(8,128)(2,1)S(1)}, u32[]{:S(2)}, u32[]{:S(2)}) collective-permute-start(bf16[1024,128]{1,0:T(8,128)(2,1)S(1)} %get-tuple-element.22.refs_0_), channel_id=1, source_target_pairs={{0,12},{2,14},{4,0},{6,2},{8,4},{10,6},{12,8},{14,10},{1,13},{3,15... | collective-permute-start | bytes 786440 | tf_op jit(solution)/shard_map/ppermute | solution.py:286
  31.3 1.9 collective-permute-start.1
  34.0 1.8 pack_y.1
  35.7 6.8 %all-to-all-start.1 = ((bf16[8,272,128]{2,1,0:T(8,128)(2,1)}), bf16[8,272,128]{2,1,0:T(8,128)(2,1)S(1)}, u32[]{:S(2)}, u32[]{:S(2)}) async-start(bf16[8,272,128]{2,1,0:T(8,128)(2,1)} %pack_y.1), calls=%async_computation.1 | async-start | bytes 1114112 | tf_op jit(solution)/shard_map/all_to_all | solution.py:278
  42.6 6.9 %collective-permute-start.6 = (bf16[1024,128]{1,0:T(8,128)(2,1)S(1)}, bf16[1024,128]{1,0:T(8,128)(2,1)S(1)}, u32[]{:S(2)}, u32[]{:S(2)}) collective-permute-start(bf16[1024,128]{1,0:T(8,128)(2,1)S(1)} %get-tuple-element.22.refs_0_), channel_id=1, source_target_pairs={{0,14},{2,0},{4,2},{6,4},{8,6},{10,8},{12,10},{14,12},{1,15},{3,1}... | collective-permute-start | bytes 786440 | tf_op jit(solution)/shard_map/ppermute | solution.py:286
  49.5 1.9 collective-permute-start
  51.4 4.6 %collective-permute-start.5 = (bf16[1024,128]{1,0:T(8,128)(2,1)S(1)}, bf16[1024,128]{1,0:T(8,128)(2,1)S(1)}, u32[]{:S(2)}, u32[]{:S(2)}) collective-permute-start(bf16[1024,128]{1,0:T(8,128)(2,1)S(1)} %collective-permute-done.4.refs_6_), channel_id=1, source_target_pairs={{0,14},{2,0},{4,2},{6,4},{8,6},{10,8},{12,10},{14,12},{1,15},{3,1}... | collective-permute-start | bytes 786440 | tf_op jit(solution)/shard_map/ppermute | solution.py:286
  56.0 1.9 collective-permute-start.3
  57.9 1.9 collective-permute-start.2
  59.9 9.4 %collective-permute-done.3.refs_4_ = bf16[1024,128]{1,0:T(8,128)(2,1)S(1)} collective-permute-done((bf16[1024,128]{1,0:T(8,128)(2,1)S(1)}, bf16[1024,128]{1,0:T(8,128)(2,1)S(1)}, u32[]{:S(2)}, u32[]{:S(2)}) %collective-permute-start.3) | collective-permute-done | bytes 262176 | tf_op jit(solution)/shard_map/ppermute | solution.py:286
  69.3 6.1 %collective-permute-done.2.refs_3_ = bf16[1024,128]{1,0:T(8,128)(2,1)S(1)} collective-permute-done((bf16[1024,128]{1,0:T(8,128)(2,1)S(1)}, bf16[1024,128]{1,0:T(8,128)(2,1)S(1)}, u32[]{:S(2)}, u32[]{:S(2)}) %collective-permute-start.2) | collective-permute-done | bytes 262176 | tf_op jit(solution)/shard_map/ppermute | solution.py:286
  75.5 4.8 %collective-permute-start.7 = (bf16[8,1024,128]{2,1,0:T(8,128)(2,1)S(1)}, bf16[8,1024,128]{2,1,0:T(8,128)(2,1)}, u32[]{:S(2)}, u32[]{:S(2)}) collective-permute-start(bf16[8,1024,128]{2,1,0:T(8,128)(2,1)S(1)} %gather_up.1.mine), channel_id=1, source_target_pairs={{0,1},{1,0},{2,3},{3,2},{4,5},{5,4},{6,7},{7,6},{8,9},{9,8},{10,11... | collective-permute-start | bytes 6291464 | tf_op jit(solution)/shard_map/ppermute | solution.py:282
  80.3 0.8 pick_arrival.1
  81.1 20.4 %all_to_all.25.late = bf16[8,256,128]{2,1,0:T(8,128)(2,1)S(1)} all-to-all(bf16[8,256,128]{2,1,0:T(8,128)(2,1)S(1)} %get-tuple-element.23), channel_id=1, replica_groups=mesh['y'=8,'x'=4,'z'=8,'c'=2] {'z'}, dimensions={0} | all-to-all | bytes 1048576 | tf_op jit(solution)/shard_map/all_to_all | solution.py:278
  101.5 2.3 %collective-permute-start.8 = (bf16[8,256,128]{2,1,0:T(8,128)(2,1)S(1)}, bf16[8,256,128]{2,1,0:T(8,128)(2,1)S(1)}, u32[]{:S(2)}, u32[]{:S(2)}) collective-permute-start(bf16[8,256,128]{2,1,0:T(8,128)(2,1)S(1)} %all_to_all.25.late), channel_id=1, source_target_pairs={{0,1},{1,0},{2,3},{3,2},{4,5},{5,4},{6,7},{7,6},{8,9},{9,8},{10,11... | collective-permute-start | bytes 1572872 | tf_op jit(solution)/shard_map/ppermute | solution.py:282
  103.9 1.5 collective-permute-done.8.late_other
  105.4 5.2 %lay_out.1 = (bf16[512,2048]{1,0:T(8,128)(2,1)}, bf16[512,2048]{1,0:T(8,128)(2,1)}) custom-call(s32[5]{0:T(128)S(1)} %stack.19.pos, s32[3,16]{1,0:T(4,128)S(1)} %bitcast.12, bf16[8,1024,128]{2,1,0:T(8,128)(2,1)S(1)} %gather_up.1.mine, bf16[8,1024,128]{2,1,0:T(8,128)(2,1)} %collective-permute-done.7.other, bf16[8,256,128]{2,1,0:T(8,128)(2,1)S(1)} %all_to_all.25.late, ...), custom_call_target="tpu_custom_call" | custom-call | tf_op jit(solution)/shard_map/lay_out/pallas_call | solution.py:352
  110.5 2.2 %all-gather.2.cloned.1.call-done.weights = bf16[2048,1536]{1,0:T(8,128)(2,1)} async-done(((bf16[64,1536]{1,0:T(8,128)(2,1)}), bf16[2048,1536]{1,0:T(8,128)(2,1)}) %all-gather.2.cloned.1.call-update) | async-done | bytes 6291472 | tf_op jit(solution)/shard_map/all_gather | solution.py:298
  112.7 9.9 %compute.1 = (bf16[512,512]{1,0:T(8,128)(2,1)}, bf16[4,8,64,768]{3,2,1,0:T(8,128)(2,1)S(1)}, bf16[8,256,768]{2,1,0:T(8,128)(2,1)}) custom-call(f32[8,128]{1,0:T(8,128)S(1)} %get-tuple-element.21.total, bf16[512,2048]{1,0:T(8,128)(2,1)} %get-tuple-element.24.tok_in, bf16[512,2048]{1,0:T(8,128)(2,1)} %get-tuple-element.25.grad_in, ...), custom_call_target="tpu_custom_call" | custom-call | tf_op jit(solution)/shard_map/compute/pallas_call | solution.py:367
  122.6 38.3 %all_to_all.26.got = bf16[4,8,64,768]{3,2,1,0:T(8,128)(2,1)S(1)} all-to-all(bf16[4,8,64,768]{3,2,1,0:T(8,128)(2,1)S(1)} %get-tuple-element.27), channel_id=1, replica_groups=mesh['y'=8,'x'=4,'z'=8,'c'=2] {'x'}, dimensions={0} | all-to-all | bytes 6291456 | tf_op jit(solution)/shard_map/all_to_all | solution.py:278
  160.9 1.3 add_x.1
  162.2 5.8 %all-to-all-start.4 = ((bf16[8,64,768]{2,1,0:T(8,128)(2,1)}), bf16[8,64,768]{2,1,0:T(8,128)(2,1)S(1)}, u32[]{:S(2)}, u32[]{:S(2)}) async-start(bf16[8,64,768]{2,1,0:T(8,128)(2,1)} %add_x.1), calls=%async_computation.4 | async-start | bytes 1572864 | tf_op jit(solution)/shard_map/all_to_all | solution.py:278
  168.1 1.0 copy-done
  169.6 2.4 %collective-permute-start.9 = (bf16[64,768]{1,0:T(8,128)(2,1)S(1)}, bf16[64,768]{1,0:T(8,128)(2,1)S(1)}, u32[]{:S(2)}, u32[]{:S(2)}) collective-permute-start(bf16[64,768]{1,0:T(8,128)(2,1)S(1)} %get-tuple-element.30), channel_id=1, source_target_pairs={{0,16},{16,32},{32,48},{48,0},{1,17},{17,33},{33,49},{49,1},{2,18}... | collective-permute-start | bytes 294920 | tf_op jit(solution)/shard_map/ppermute | solution.py:417
  172.1 4.4 %collective-permute-start.10 = (bf16[64,768]{1,0:T(8,128)(2,1)S(1)}, bf16[64,768]{1,0:T(8,128)(2,1)S(1)}, u32[]{:S(2)}, u32[]{:S(2)}) collective-permute-start(bf16[64,768]{1,0:T(8,128)(2,1)S(1)} %get-tuple-element.31), channel_id=1, source_target_pairs={{0,32},{16,48},{32,0},{48,16},{1,33},{17,49},{33,1},{49,17},{2,34}... | collective-permute-start | bytes 294920 | tf_op jit(solution)/shard_map/ppermute | solution.py:417
  176.4 3.0 %collective-permute-start.11 = (bf16[64,768]{1,0:T(8,128)(2,1)S(1)}, bf16[64,768]{1,0:T(8,128)(2,1)S(1)}, u32[]{:S(2)}, u32[]{:S(2)}) collective-permute-start(bf16[64,768]{1,0:T(8,128)(2,1)S(1)} %get-tuple-element.32), channel_id=1, source_target_pairs={{0,48},{16,0},{32,16},{48,32},{1,49},{17,1},{33,17},{49,33},{2,50}... | collective-permute-start | bytes 294920 | tf_op jit(solution)/shard_map/ppermute | solution.py:417
  179.5 10.6 %all-to-all-done.4.from_y = bf16[8,64,768]{2,1,0:T(8,128)(2,1)S(1)} async-done(((bf16[8,64,768]{2,1,0:T(8,128)(2,1)}), bf16[8,64,768]{2,1,0:T(8,128)(2,1)S(1)}, u32[]{:S(2)}, u32[]{:S(2)}) %all-to-all-start.4) | async-done | bytes 786464 | tf_op jit(solution)/shard_map/all_to_all | solution.py:278
  (31 shorter events, 3.8 us)
Async XLA Ops:
  7.2 105.5 %all-gather.2.cloned.1.call-start = ((), (), s32[]{:S(2)}) async-start(), calls=%async_computation.6 | async-start | bytes 6488064 | tf_op jit(solution)/shard_map/all_gather | solution.py:298
  9.6 0.9 copy-start.1
  10.5 0.9 copy-start.2
  11.4 0.7 copy-start.3
  12.1 0.7 copy-start.6
  15.7 64.5 %copy-start.5 = (s32[16,3]{0,1:T(4,128)S(1)}, s32[16,3]{0,1:T(4,128)}, u32[]{:S(2)}) copy-start(s32[16,3]{0,1:T(4,128)} %param.11) | copy-start | bytes 580
  15.7 17.5 %all-to-all-start = ((bf16[4,528,128]{2,1,0:T(8,128)(2,1)}), bf16[4,528,128]{2,1,0:T(8,128)(2,1)S(1)}, u32[]{:S(2)}, u32[]{:S(2)}) async-start(bf16[4,528,128]{2,1,0:T(8,128)(2,1)} %get-tuple-element.20), calls=%async_computation | async-start | bytes 1081344 | tf_op jit(solution)/shard_map/all_to_all | solution.py:278
  20.7 30.7 %collective-permute-start.4 = (bf16[1024,128]{1,0:T(8,128)(2,1)S(1)}, bf16[1024,128]{1,0:T(8,128)(2,1)S(1)}, u32[]{:S(2)}, u32[]{:S(2)}) collective-permute-start(bf16[1024,128]{1,0:T(8,128)(2,1)S(1)} %get-tuple-element.22.refs_0_), channel_id=1, source_target_pairs={{0,12},{2,14},{4,0},{6,2},{8,4},{10,6},{12,8},{14,10},{1,13},{3,15... | collective-permute-start | bytes 786440 | tf_op jit(solution)/shard_map/ppermute | solution.py:286
  31.3 24.7 %collective-permute-start.1 = (bf16[1024,128]{1,0:T(8,128)(2,1)S(1)}, bf16[1024,128]{1,0:T(8,128)(2,1)S(1)}, u32[]{:S(2)}, u32[]{:S(2)}) collective-permute-start(bf16[1024,128]{1,0:T(8,128)(2,1)S(1)} %get-tuple-element.22.refs_0_), channel_id=1, source_target_pairs={{0,4},{2,6},{4,8},{6,10},{8,12},{10,14},{12,0},{14,2},{1,5},{3,7},... | collective-permute-start | bytes 786440 | tf_op jit(solution)/shard_map/ppermute | solution.py:286
  33.3 0.7 copy-start.4
  35.7 44.5 %all-to-all-start.1 = ((bf16[8,272,128]{2,1,0:T(8,128)(2,1)}), bf16[8,272,128]{2,1,0:T(8,128)(2,1)S(1)}, u32[]{:S(2)}, u32[]{:S(2)}) async-start(bf16[8,272,128]{2,1,0:T(8,128)(2,1)} %pack_y.1), calls=%async_computation.1 | async-start | bytes 1114112 | tf_op jit(solution)/shard_map/all_to_all | solution.py:278
  42.6 125.5 %reduce-scatter.2.cloned.1.call-start = ((), (), s32[]{:S(2)}) async-start(), calls=%async_computation.7 | async-start | bytes 3538944 | tf_op jit(solution)/shard_map/reduce_scatter | solution.py:396
  42.6 17.3 %collective-permute-start.6 = (bf16[1024,128]{1,0:T(8,128)(2,1)S(1)}, bf16[1024,128]{1,0:T(8,128)(2,1)S(1)}, u32[]{:S(2)}, u32[]{:S(2)}) collective-permute-start(bf16[1024,128]{1,0:T(8,128)(2,1)S(1)} %get-tuple-element.22.refs_0_), channel_id=1, source_target_pairs={{0,14},{2,0},{4,2},{6,4},{8,6},{10,8},{12,10},{14,12},{1,15},{3,1}... | collective-permute-start | bytes 786440 | tf_op jit(solution)/shard_map/ppermute | solution.py:286
  49.5 10.4 %collective-permute-start = (bf16[1024,128]{1,0:T(8,128)(2,1)S(1)}, bf16[1024,128]{1,0:T(8,128)(2,1)S(1)}, u32[]{:S(2)}, u32[]{:S(2)}) collective-permute-start(bf16[1024,128]{1,0:T(8,128)(2,1)S(1)} %get-tuple-element.22.refs_0_), channel_id=1, source_target_pairs={{0,2},{2,4},{4,6},{6,8},{8,10},{10,12},{12,14},{14,0},{1,3},{3,5},... | collective-permute-start | bytes 786440 | tf_op jit(solution)/shard_map/ppermute | solution.py:286
  51.4 8.5 %collective-permute-start.5 = (bf16[1024,128]{1,0:T(8,128)(2,1)S(1)}, bf16[1024,128]{1,0:T(8,128)(2,1)S(1)}, u32[]{:S(2)}, u32[]{:S(2)}) collective-permute-start(bf16[1024,128]{1,0:T(8,128)(2,1)S(1)} %collective-permute-done.4.refs_6_), channel_id=1, source_target_pairs={{0,14},{2,0},{4,2},{6,4},{8,6},{10,8},{12,10},{14,12},{1,15},{3,1}... | collective-permute-start | bytes 786440 | tf_op jit(solution)/shard_map/ppermute | solution.py:286
  56.0 13.3 %collective-permute-start.3 = (bf16[1024,128]{1,0:T(8,128)(2,1)S(1)}, bf16[1024,128]{1,0:T(8,128)(2,1)S(1)}, u32[]{:S(2)}, u32[]{:S(2)}) collective-permute-start(bf16[1024,128]{1,0:T(8,128)(2,1)S(1)} %collective-permute-done.1.refs_2_), channel_id=1, source_target_pairs={{0,4},{2,6},{4,8},{6,10},{8,12},{10,14},{12,0},{14,2},{1,5},{3,7},... | collective-permute-start | bytes 786440 | tf_op jit(solution)/shard_map/ppermute | solution.py:286
  57.9 17.4 %collective-permute-start.2 = (bf16[1024,128]{1,0:T(8,128)(2,1)S(1)}, bf16[1024,128]{1,0:T(8,128)(2,1)S(1)}, u32[]{:S(2)}, u32[]{:S(2)}) collective-permute-start(bf16[1024,128]{1,0:T(8,128)(2,1)S(1)} %collective-permute-done.1.refs_2_), channel_id=1, source_target_pairs={{0,2},{2,4},{4,6},{6,8},{8,10},{10,12},{12,14},{14,0},{1,3},{3,5},... | collective-permute-start | bytes 786440 | tf_op jit(solution)/shard_map/ppermute | solution.py:286
  75.5 28.4 %collective-permute-start.7 = (bf16[8,1024,128]{2,1,0:T(8,128)(2,1)S(1)}, bf16[8,1024,128]{2,1,0:T(8,128)(2,1)}, u32[]{:S(2)}, u32[]{:S(2)}) collective-permute-start(bf16[8,1024,128]{2,1,0:T(8,128)(2,1)S(1)} %gather_up.1.mine), channel_id=1, source_target_pairs={{0,1},{1,0},{2,3},{3,2},{4,5},{5,4},{6,7},{7,6},{8,9},{9,8},{10,11... | collective-permute-start | bytes 6291464 | tf_op jit(solution)/shard_map/ppermute | solution.py:282
  101.5 3.9 %collective-permute-start.8 = (bf16[8,256,128]{2,1,0:T(8,128)(2,1)S(1)}, bf16[8,256,128]{2,1,0:T(8,128)(2,1)S(1)}, u32[]{:S(2)}, u32[]{:S(2)}) collective-permute-start(bf16[8,256,128]{2,1,0:T(8,128)(2,1)S(1)} %all_to_all.25.late), channel_id=1, source_target_pairs={{0,1},{1,0},{2,3},{3,2},{4,5},{5,4},{6,7},{7,6},{8,9},{9,8},{10,11... | collective-permute-start | bytes 1572872 | tf_op jit(solution)/shard_map/ppermute | solution.py:282
  162.2 27.8 %all-to-all-start.4 = ((bf16[8,64,768]{2,1,0:T(8,128)(2,1)}), bf16[8,64,768]{2,1,0:T(8,128)(2,1)S(1)}, u32[]{:S(2)}, u32[]{:S(2)}) async-start(bf16[8,64,768]{2,1,0:T(8,128)(2,1)} %add_x.1), calls=%async_computation.4 | async-start | bytes 1572864 | tf_op jit(solution)/shard_map/all_to_all | solution.py:278
  168.1 1.0 copy-start
  169.6 20.4 %collective-permute-start.9 = (bf16[64,768]{1,0:T(8,128)(2,1)S(1)}, bf16[64,768]{1,0:T(8,128)(2,1)S(1)}, u32[]{:S(2)}, u32[]{:S(2)}) collective-permute-start(bf16[64,768]{1,0:T(8,128)(2,1)S(1)} %get-tuple-element.30), channel_id=1, source_target_pairs={{0,16},{16,32},{32,48},{48,0},{1,17},{17,33},{33,49},{49,1},{2,18}... | collective-permute-start | bytes 294920 | tf_op jit(solution)/shard_map/ppermute | solution.py:417
  172.1 18.0 %collective-permute-start.10 = (bf16[64,768]{1,0:T(8,128)(2,1)S(1)}, bf16[64,768]{1,0:T(8,128)(2,1)S(1)}, u32[]{:S(2)}, u32[]{:S(2)}) collective-permute-start(bf16[64,768]{1,0:T(8,128)(2,1)S(1)} %get-tuple-element.31), channel_id=1, source_target_pairs={{0,32},{16,48},{32,0},{48,16},{1,33},{17,49},{33,1},{49,17},{2,34}... | collective-permute-start | bytes 294920 | tf_op jit(solution)/shard_map/ppermute | solution.py:417
  176.4 13.6 %collective-permute-start.11 = (bf16[64,768]{1,0:T(8,128)(2,1)S(1)}, bf16[64,768]{1,0:T(8,128)(2,1)S(1)}, u32[]{:S(2)}, u32[]{:S(2)}) collective-permute-start(bf16[64,768]{1,0:T(8,128)(2,1)S(1)} %get-tuple-element.32), channel_id=1, source_target_pairs={{0,48},{16,0},{32,16},{48,32},{1,49},{17,1},{33,17},{49,33},{2,50}... | collective-permute-start | bytes 294920 | tf_op jit(solution)/shard_map/ppermute | solution.py:417
Sparse Core Ops, SparseCore 0:
  11.7 100.9 all-gather.1
  122.8 44.6 reduce-scatter.1

commit v4 on v3

--- a/solution.py
+++ b/solution.py
@@ -258,20 +258,25 @@
         out[...] = part[(pos[1] + k) % NX]
 
 
-def finish(from_y, *refs):
-    parts, (gate, up, down) = refs[:NX], refs[NX:]
+def finish_x(*refs):
+    parts, (rest, down) = refs[:NX], refs[NX:]
+    acc = parts[0][...].astype(jnp.float32)
+    for part in parts[1:]:
+        acc = acc + part[...].astype(jnp.float32)
+    cut = rest.shape[1]
+    rest[...] = acc[:, :cut]
+    down[...] = acc[:, cut:]
+
+
+def finish(from_y, rest, gate, up):
     acc = from_y[0].astype(jnp.float32)
     for i in range(1, NY):
         acc = acc + from_y[i].astype(jnp.float32)
-    bcc = parts[0][...].astype(jnp.float32)
-    for part in parts[1:]:
-        bcc = bcc + part[...].astype(jnp.float32)
     width = up.shape[1]
     cut = acc.shape[1] - width
     up[...] = acc[:, :width]
     gate[:, :cut] = acc[:, width:]
-    gate[:, cut:] = bcc[:, : width - cut]
-    down[...] = bcc[:, width - cut :]
+    gate[:, cut:] = rest[...]
 
 
 def a2a(value, axis):
@@ -416,14 +421,25 @@
     from_x = [turned[0]] + [
         lax.ppermute(turned[k], "x", [(i, (i + k) % NX) for i in range(NX)]) for k in range(1, NX)
     ]
-    gate_grad, up_grad, down_grad = pl.pallas_call(
+    rest, down_grad = pl.pallas_call(
+        finish_x,
+        out_shape=(
+            jax.ShapeDtypeStruct((per, hid - CUT), f32),
+            jax.ShapeDtypeStruct((per, hid), f32),
+        ),
+        in_specs=[vmem()] * NX,
+        out_specs=(vmem(), vmem()),
+        compiler_params=params(8),
+        name="finish_x",
+    )(*from_x)
+    gate_grad, up_grad = pl.pallas_call(
         finish,
-        out_shape=tuple(jax.ShapeDtypeStruct((per, hid), f32) for _ in range(3)),
-        in_specs=[vmem()] * (NX + 1),
-        out_specs=(vmem(), vmem(), vmem()),
+        out_shape=tuple(jax.ShapeDtypeStruct((per, hid), f32) for _ in range(2)),
+        in_specs=[vmem(), vmem()],
+        out_specs=(vmem(), vmem()),
         compiler_params=params(8),
         name="finish",
-    )(from_y, *from_x)
+    )(from_y, rest)
     return (hidden, gate_grad, up_grad, down_grad)
 
 

time: 199 us -> 199 us (level)
    all_to_all x3, waiting for transfers between devices: 10.6 us -> 7.22 us  [a2a(): return lax.all_to_all(value, axis, split_axis=0, concat_axis=0, tiled=True)]
    ppermute x3, waiting for transfers between devices: 0.01 us -> 2.52 us  [step(): lax.ppermute(turned[k], 'x', [(i, (i + k) % NX) for i in range(NX)])]
  transfers between devices with their start and end apart: 17 -> 17, of which waited for: 5 -> 6; matrix products, arithmetic and copies ran while one was open for 0% -> 0% of each run, Pallas kernels for 6% -> 7%
where the time goes in v4:
time: 199 us; the launch traced here: 198 us
  starting transfers between devices  64.5 us (32%)
  blocking collectives  58.7 us (29%)
  waiting for transfers between devices  28.9 us (15%)
  Pallas kernels  24 us (12%)
  between operations  14.9 us (7%)
  local copies, waits for them, and re-layouts  4.98 us (3%)
    all_to_all x2, blocking collectives, a2a(): return lax.all_to_all(value, axis, split_axis=0, concat_axis=0, tiled=True)  58.7 us
    ppermute x7, starting transfers between devices, along_z(): return lax.ppermute(value, 'z', [(i, (i + by) % NZ) for i in range(NZ)])  29.8 us
    all_to_all x3, starting transfers between devices, a2a(): return lax.all_to_all(value, axis, split_axis=0, concat_axis=0, tiled=True)  17.6 us
    ppermute x7, waiting for transfers between devices, along_z(): return lax.ppermute(value, 'z', [(i, (i + by) % NZ) for i in range(NZ)])  15.4 us
    ppermute x3, starting transfers between devices, step(): lax.ppermute(turned[k], 'x', [(i, (i + k) % NX) for i in range(NX)])  9.93 us
    pallas_call x1, Pallas kernels, step(): pl.pallas_call(compute, out_shape=(pltpu.HBM((span, hid), bf), pltpu.VMEM...  9.9 us
    all_to_all x3, waiting for transfers between devices, a2a(): return lax.all_to_all(value, axis, split_axis=0, concat_axis=0, tiled=True)  7.22 us
    ppermute x2, starting transfers between devices, swap(): return lax.ppermute(value, 'c', [(0, 1), (1, 0)])  7.09 us
  transfers between devices with their start and end apart: 17, of which 6 were waited for; matrix products, arithmetic and copies ran while one was open for 0% of the time, Pallas kernels for 7%

profile of v4, /device:TPU:1, one launch (start us, length us, event | category | flops | bytes accessed | tf_op | source)
XLA Modules:
  0.0 197.6 jit_solution(3711060847512305146)
XLA Ops:
  7.2 1.6 pad_maximum_fusion
  9.6 0.9 copy-done.1
  10.5 0.9 copy-done.2
  12.8 2.9 %pack_x.1 = (bf16[4,528,128]{2,1,0:T(8,128)(2,1)}, bf16[1024,128]{1,0:T(8,128)(2,1)S(1)}) custom-call(s32[5]{0:T(128)S(1)} %stack.19.pos, s32[3,16]{1,0:T(4,128)S(1)} %bitcast.9, s32[6,128]{1,0:T(8,128)S(1)} %bitcast.13, bf16[768,128]{1,0:T(8,128)(2,1)S(1)} %copy-done.1, bf16[768,128]{1,0:T(8,128)(2,1)S(1)} %copy-done.2), custom_call_target="tpu_custom_call" | custom-call | tf_op jit(solution)/shard_map/pack_x/pallas_call | solution.py:308
  15.7 4.9 %all-to-all-start = ((bf16[4,528,128]{2,1,0:T(8,128)(2,1)}), bf16[4,528,128]{2,1,0:T(8,128)(2,1)S(1)}, u32[]{:S(2)}, u32[]{:S(2)}) async-start(bf16[4,528,128]{2,1,0:T(8,128)(2,1)} %get-tuple-element.21), calls=%async_computation | async-start | bytes 1081344 | tf_op jit(solution)/shard_map/all_to_all | solution.py:283
  20.7 10.6 %collective-permute-start.4 = (bf16[1024,128]{1,0:T(8,128)(2,1)S(1)}, bf16[1024,128]{1,0:T(8,128)(2,1)S(1)}, u32[]{:S(2)}, u32[]{:S(2)}) collective-permute-start(bf16[1024,128]{1,0:T(8,128)(2,1)S(1)} %get-tuple-element.23.refs_0_), channel_id=1, source_target_pairs={{0,12},{2,14},{4,0},{6,2},{8,4},{10,6},{12,8},{14,10},{1,13},{3,15... | collective-permute-start | bytes 786440 | tf_op jit(solution)/shard_map/ppermute | solution.py:291
  31.3 1.9 collective-permute-start.1
  34.0 1.8 pack_y.1
  35.7 6.8 %all-to-all-start.1 = ((bf16[8,272,128]{2,1,0:T(8,128)(2,1)}), bf16[8,272,128]{2,1,0:T(8,128)(2,1)S(1)}, u32[]{:S(2)}, u32[]{:S(2)}) async-start(bf16[8,272,128]{2,1,0:T(8,128)(2,1)} %pack_y.1), calls=%async_computation.1 | async-start | bytes 1114112 | tf_op jit(solution)/shard_map/all_to_all | solution.py:283
  42.6 6.9 %collective-permute-start.6 = (bf16[1024,128]{1,0:T(8,128)(2,1)S(1)}, bf16[1024,128]{1,0:T(8,128)(2,1)S(1)}, u32[]{:S(2)}, u32[]{:S(2)}) collective-permute-start(bf16[1024,128]{1,0:T(8,128)(2,1)S(1)} %get-tuple-element.23.refs_0_), channel_id=1, source_target_pairs={{0,14},{2,0},{4,2},{6,4},{8,6},{10,8},{12,10},{14,12},{1,15},{3,1}... | collective-permute-start | bytes 786440 | tf_op jit(solution)/shard_map/ppermute | solution.py:291
  49.5 1.9 collective-permute-start
  51.4 4.6 %collective-permute-start.5 = (bf16[1024,128]{1,0:T(8,128)(2,1)S(1)}, bf16[1024,128]{1,0:T(8,128)(2,1)S(1)}, u32[]{:S(2)}, u32[]{:S(2)}) collective-permute-start(bf16[1024,128]{1,0:T(8,128)(2,1)S(1)} %collective-permute-done.4.refs_6_), channel_id=1, source_target_pairs={{0,14},{2,0},{4,2},{6,4},{8,6},{10,8},{12,10},{14,12},{1,15},{3,1}... | collective-permute-start | bytes 786440 | tf_op jit(solution)/shard_map/ppermute | solution.py:291
  56.0 1.9 collective-permute-start.3
  57.9 1.9 collective-permute-start.2
  59.9 9.4 %collective-permute-done.3.refs_4_ = bf16[1024,128]{1,0:T(8,128)(2,1)S(1)} collective-permute-done((bf16[1024,128]{1,0:T(8,128)(2,1)S(1)}, bf16[1024,128]{1,0:T(8,128)(2,1)S(1)}, u32[]{:S(2)}, u32[]{:S(2)}) %collective-permute-start.3) | collective-permute-done | bytes 262176 | tf_op jit(solution)/shard_map/ppermute | solution.py:291
  69.3 6.1 %collective-permute-done.2.refs_3_ = bf16[1024,128]{1,0:T(8,128)(2,1)S(1)} collective-permute-done((bf16[1024,128]{1,0:T(8,128)(2,1)S(1)}, bf16[1024,128]{1,0:T(8,128)(2,1)S(1)}, u32[]{:S(2)}, u32[]{:S(2)}) %collective-permute-start.2) | collective-permute-done | bytes 262176 | tf_op jit(solution)/shard_map/ppermute | solution.py:291
  75.5 4.8 %collective-permute-start.7 = (bf16[8,1024,128]{2,1,0:T(8,128)(2,1)S(1)}, bf16[8,1024,128]{2,1,0:T(8,128)(2,1)}, u32[]{:S(2)}, u32[]{:S(2)}) collective-permute-start(bf16[8,1024,128]{2,1,0:T(8,128)(2,1)S(1)} %gather_up.1.mine), channel_id=1, source_target_pairs={{0,1},{1,0},{2,3},{3,2},{4,5},{5,4},{6,7},{7,6},{8,9},{9,8},{10,11... | collective-permute-start | bytes 6291464 | tf_op jit(solution)/shard_map/ppermute | solution.py:287
  81.1 20.4 %all_to_all.25.late = bf16[8,256,128]{2,1,0:T(8,128)(2,1)S(1)} all-to-all(bf16[8,256,128]{2,1,0:T(8,128)(2,1)S(1)} %get-tuple-element.24), channel_id=1, replica_groups=mesh['y'=8,'x'=4,'z'=8,'c'=2] {'z'}, dimensions={0} | all-to-all | bytes 1048576 | tf_op jit(solution)/shard_map/all_to_all | solution.py:283
  101.5 2.3 %collective-permute-start.8 = (bf16[8,256,128]{2,1,0:T(8,128)(2,1)S(1)}, bf16[8,256,128]{2,1,0:T(8,128)(2,1)S(1)}, u32[]{:S(2)}, u32[]{:S(2)}) collective-permute-start(bf16[8,256,128]{2,1,0:T(8,128)(2,1)S(1)} %all_to_all.25.late), channel_id=1, source_target_pairs={{0,1},{1,0},{2,3},{3,2},{4,5},{5,4},{6,7},{7,6},{8,9},{9,8},{10,11... | collective-permute-start | bytes 1572872 | tf_op jit(solution)/shard_map/ppermute | solution.py:287
  103.8 1.5 collective-permute-done.8.late_other
  105.3 5.1 %lay_out.1 = (bf16[512,2048]{1,0:T(8,128)(2,1)}, bf16[512,2048]{1,0:T(8,128)(2,1)}) custom-call(s32[5]{0:T(128)S(1)} %stack.19.pos, s32[3,16]{1,0:T(4,128)S(1)} %bitcast.12, bf16[8,1024,128]{2,1,0:T(8,128)(2,1)S(1)} %gather_up.1.mine, bf16[8,1024,128]{2,1,0:T(8,128)(2,1)} %collective-permute-done.7.other, bf16[8,256,128]{2,1,0:T(8,128)(2,1)S(1)} %all_to_all.25.late, ...), custom_call_target="tpu_custom_call" | custom-call | tf_op jit(solution)/shard_map/lay_out/pallas_call | solution.py:357
  110.5 2.2 %all-gather.2.cloned.1.call-done.weights = bf16[2048,1536]{1,0:T(8,128)(2,1)} async-done(((bf16[64,1536]{1,0:T(8,128)(2,1)}), bf16[2048,1536]{1,0:T(8,128)(2,1)}) %all-gather.2.cloned.1.call-update) | async-done | bytes 6291472 | tf_op jit(solution)/shard_map/all_gather | solution.py:303
  112.7 9.9 %compute.1 = (bf16[512,512]{1,0:T(8,128)(2,1)}, bf16[4,8,64,768]{3,2,1,0:T(8,128)(2,1)S(1)}, bf16[8,256,768]{2,1,0:T(8,128)(2,1)}) custom-call(f32[8,128]{1,0:T(8,128)S(1)} %get-tuple-element.22.total, bf16[512,2048]{1,0:T(8,128)(2,1)} %get-tuple-element.25.tok_in, bf16[512,2048]{1,0:T(8,128)(2,1)} %get-tuple-element.26.grad_in, ...), custom_call_target="tpu_custom_call" | custom-call | tf_op jit(solution)/shard_map/compute/pallas_call | solution.py:372
  122.6 38.3 %all_to_all.26.got = bf16[4,8,64,768]{3,2,1,0:T(8,128)(2,1)S(1)} all-to-all(bf16[4,8,64,768]{3,2,1,0:T(8,128)(2,1)S(1)} %get-tuple-element.28), channel_id=1, replica_groups=mesh['y'=8,'x'=4,'z'=8,'c'=2] {'x'}, dimensions={0} | all-to-all | bytes 6291456 | tf_op jit(solution)/shard_map/all_to_all | solution.py:283
  160.9 1.3 add_x.1
  162.1 5.9 %all-to-all-start.4 = ((bf16[8,64,768]{2,1,0:T(8,128)(2,1)}), bf16[8,64,768]{2,1,0:T(8,128)(2,1)S(1)}, u32[]{:S(2)}, u32[]{:S(2)}) async-start(bf16[8,64,768]{2,1,0:T(8,128)(2,1)} %add_x.1), calls=%async_computation.4 | async-start | bytes 1572864 | tf_op jit(solution)/shard_map/all_to_all | solution.py:283
  168.0 1.0 copy-done
  169.6 2.3 %collective-permute-start.9 = (bf16[64,768]{1,0:T(8,128)(2,1)S(1)}, bf16[64,768]{1,0:T(8,128)(2,1)S(1)}, u32[]{:S(2)}, u32[]{:S(2)}) collective-permute-start(bf16[64,768]{1,0:T(8,128)(2,1)S(1)} %get-tuple-element.31), channel_id=1, source_target_pairs={{0,16},{16,32},{32,48},{48,0},{1,17},{17,33},{33,49},{49,1},{2,18}... | collective-permute-start | bytes 294920 | tf_op jit(solution)/shard_map/ppermute | solution.py:422
  171.9 4.5 %collective-permute-start.10 = (bf16[64,768]{1,0:T(8,128)(2,1)S(1)}, bf16[64,768]{1,0:T(8,128)(2,1)S(1)}, u32[]{:S(2)}, u32[]{:S(2)}) collective-permute-start(bf16[64,768]{1,0:T(8,128)(2,1)S(1)} %get-tuple-element.32), channel_id=1, source_target_pairs={{0,32},{16,48},{32,0},{48,16},{1,33},{17,49},{33,1},{49,17},{2,34}... | collective-permute-start | bytes 294920 | tf_op jit(solution)/shard_map/ppermute | solution.py:422
  176.4 3.1 %collective-permute-start.11 = (bf16[64,768]{1,0:T(8,128)(2,1)S(1)}, bf16[64,768]{1,0:T(8,128)(2,1)S(1)}, u32[]{:S(2)}, u32[]{:S(2)}) collective-permute-start(bf16[64,768]{1,0:T(8,128)(2,1)S(1)} %get-tuple-element.33), channel_id=1, source_target_pairs={{0,48},{16,0},{32,16},{48,32},{1,49},{17,1},{33,17},{49,33},{2,50}... | collective-permute-start | bytes 294920 | tf_op jit(solution)/shard_map/ppermute | solution.py:422
  179.6 2.5 %collective-permute-done.11.refs_3_ = bf16[64,768]{1,0:T(8,128)(2,1)S(1)} collective-permute-done((bf16[64,768]{1,0:T(8,128)(2,1)S(1)}, bf16[64,768]{1,0:T(8,128)(2,1)S(1)}, u32[]{:S(2)}, u32[]{:S(2)}) %collective-permute-start.11) | collective-permute-done | bytes 98336 | tf_op jit(solution)/shard_map/ppermute | solution.py:422
  182.8 7.2 %all-to-all-done.4.from_y = bf16[8,64,768]{2,1,0:T(8,128)(2,1)S(1)} async-done(((bf16[8,64,768]{2,1,0:T(8,128)(2,1)}), bf16[8,64,768]{2,1,0:T(8,128)(2,1)S(1)}, u32[]{:S(2)}, u32[]{:S(2)}) %all-to-all-start.4) | async-done | bytes 786464 | tf_op jit(solution)/shard_map/all_to_all | solution.py:283
  (32 shorter events, 5.3 us)
Async XLA Ops:
  7.2 105.5 %all-gather.2.cloned.1.call-start = ((), (), s32[]{:S(2)}) async-start(), calls=%async_computation.6 | async-start | bytes 6488064 | tf_op jit(solution)/shard_map/all_gather | solution.py:303
  9.6 0.9 copy-start.1
  10.5 0.9 copy-start.2
  11.4 0.7 copy-start.3
  12.1 0.7 copy-start.6
  15.7 64.5 %copy-start.5 = (s32[16,3]{0,1:T(4,128)S(1)}, s32[16,3]{0,1:T(4,128)}, u32[]{:S(2)}) copy-start(s32[16,3]{0,1:T(4,128)} %param.11) | copy-start | bytes 580
  15.7 17.5 %all-to-all-start = ((bf16[4,528,128]{2,1,0:T(8,128)(2,1)}), bf16[4,528,128]{2,1,0:T(8,128)(2,1)S(1)}, u32[]{:S(2)}, u32[]{:S(2)}) async-start(bf16[4,528,128]{2,1,0:T(8,128)(2,1)} %get-tuple-element.21), calls=%async_computation | async-start | bytes 1081344 | tf_op jit(solution)/shard_map/all_to_all | solution.py:283
  20.7 30.7 %collective-permute-start.4 = (bf16[1024,128]{1,0:T(8,128)(2,1)S(1)}, bf16[1024,128]{1,0:T(8,128)(2,1)S(1)}, u32[]{:S(2)}, u32[]{:S(2)}) collective-permute-start(bf16[1024,128]{1,0:T(8,128)(2,1)S(1)} %get-tuple-element.23.refs_0_), channel_id=1, source_target_pairs={{0,12},{2,14},{4,0},{6,2},{8,4},{10,6},{12,8},{14,10},{1,13},{3,15... | collective-permute-start | bytes 786440 | tf_op jit(solution)/shard_map/ppermute | solution.py:291
  31.3 24.7 %collective-permute-start.1 = (bf16[1024,128]{1,0:T(8,128)(2,1)S(1)}, bf16[1024,128]{1,0:T(8,128)(2,1)S(1)}, u32[]{:S(2)}, u32[]{:S(2)}) collective-permute-start(bf16[1024,128]{1,0:T(8,128)(2,1)S(1)} %get-tuple-element.23.refs_0_), channel_id=1, source_target_pairs={{0,4},{2,6},{4,8},{6,10},{8,12},{10,14},{12,0},{14,2},{1,5},{3,7},... | collective-permute-start | bytes 786440 | tf_op jit(solution)/shard_map/ppermute | solution.py:291
  33.3 0.7 copy-start.4
  35.7 44.5 %all-to-all-start.1 = ((bf16[8,272,128]{2,1,0:T(8,128)(2,1)}), bf16[8,272,128]{2,1,0:T(8,128)(2,1)S(1)}, u32[]{:S(2)}, u32[]{:S(2)}) async-start(bf16[8,272,128]{2,1,0:T(8,128)(2,1)} %pack_y.1), calls=%async_computation.1 | async-start | bytes 1114112 | tf_op jit(solution)/shard_map/all_to_all | solution.py:283
  42.5 125.5 %reduce-scatter.2.cloned.1.call-start = ((), (), s32[]{:S(2)}) async-start(), calls=%async_computation.7 | async-start | bytes 3538944 | tf_op jit(solution)/shard_map/reduce_scatter | solution.py:401
  42.6 17.3 %collective-permute-start.6 = (bf16[1024,128]{1,0:T(8,128)(2,1)S(1)}, bf16[1024,128]{1,0:T(8,128)(2,1)S(1)}, u32[]{:S(2)}, u32[]{:S(2)}) collective-permute-start(bf16[1024,128]{1,0:T(8,128)(2,1)S(1)} %get-tuple-element.23.refs_0_), channel_id=1, source_target_pairs={{0,14},{2,0},{4,2},{6,4},{8,6},{10,8},{12,10},{14,12},{1,15},{3,1}... | collective-permute-start | bytes 786440 | tf_op jit(solution)/shard_map/ppermute | solution.py:291
  49.5 10.4 %collective-permute-start = (bf16[1024,128]{1,0:T(8,128)(2,1)S(1)}, bf16[1024,128]{1,0:T(8,128)(2,1)S(1)}, u32[]{:S(2)}, u32[]{:S(2)}) collective-permute-start(bf16[1024,128]{1,0:T(8,128)(2,1)S(1)} %get-tuple-element.23.refs_0_), channel_id=1, source_target_pairs={{0,2},{2,4},{4,6},{6,8},{8,10},{10,12},{12,14},{14,0},{1,3},{3,5},... | collective-permute-start | bytes 786440 | tf_op jit(solution)/shard_map/ppermute | solution.py:291
  51.4 8.5 %collective-permute-start.5 = (bf16[1024,128]{1,0:T(8,128)(2,1)S(1)}, bf16[1024,128]{1,0:T(8,128)(2,1)S(1)}, u32[]{:S(2)}, u32[]{:S(2)}) collective-permute-start(bf16[1024,128]{1,0:T(8,128)(2,1)S(1)} %collective-permute-done.4.refs_6_), channel_id=1, source_target_pairs={{0,14},{2,0},{4,2},{6,4},{8,6},{10,8},{12,10},{14,12},{1,15},{3,1}... | collective-permute-start | bytes 786440 | tf_op jit(solution)/shard_map/ppermute | solution.py:291
  56.0 13.3 %collective-permute-start.3 = (bf16[1024,128]{1,0:T(8,128)(2,1)S(1)}, bf16[1024,128]{1,0:T(8,128)(2,1)S(1)}, u32[]{:S(2)}, u32[]{:S(2)}) collective-permute-start(bf16[1024,128]{1,0:T(8,128)(2,1)S(1)} %collective-permute-done.1.refs_2_), channel_id=1, source_target_pairs={{0,4},{2,6},{4,8},{6,10},{8,12},{10,14},{12,0},{14,2},{1,5},{3,7},... | collective-permute-start | bytes 786440 | tf_op jit(solution)/shard_map/ppermute | solution.py:291
  57.9 17.4 %collective-permute-start.2 = (bf16[1024,128]{1,0:T(8,128)(2,1)S(1)}, bf16[1024,128]{1,0:T(8,128)(2,1)S(1)}, u32[]{:S(2)}, u32[]{:S(2)}) collective-permute-start(bf16[1024,128]{1,0:T(8,128)(2,1)S(1)} %collective-permute-done.1.refs_2_), channel_id=1, source_target_pairs={{0,2},{2,4},{4,6},{6,8},{8,10},{10,12},{12,14},{14,0},{1,3},{3,5},... | collective-permute-start | bytes 786440 | tf_op jit(solution)/shard_map/ppermute | solution.py:291
  75.5 28.4 %collective-permute-start.7 = (bf16[8,1024,128]{2,1,0:T(8,128)(2,1)S(1)}, bf16[8,1024,128]{2,1,0:T(8,128)(2,1)}, u32[]{:S(2)}, u32[]{:S(2)}) collective-permute-start(bf16[8,1024,128]{2,1,0:T(8,128)(2,1)S(1)} %gather_up.1.mine), channel_id=1, source_target_pairs={{0,1},{1,0},{2,3},{3,2},{4,5},{5,4},{6,7},{7,6},{8,9},{9,8},{10,11... | collective-permute-start | bytes 6291464 | tf_op jit(solution)/shard_map/ppermute | solution.py:287
  101.5 3.9 %collective-permute-start.8 = (bf16[8,256,128]{2,1,0:T(8,128)(2,1)S(1)}, bf16[8,256,128]{2,1,0:T(8,128)(2,1)S(1)}, u32[]{:S(2)}, u32[]{:S(2)}) collective-permute-start(bf16[8,256,128]{2,1,0:T(8,128)(2,1)S(1)} %all_to_all.25.late), channel_id=1, source_target_pairs={{0,1},{1,0},{2,3},{3,2},{4,5},{5,4},{6,7},{7,6},{8,9},{9,8},{10,11... | collective-permute-start | bytes 1572872 | tf_op jit(solution)/shard_map/ppermute | solution.py:287
  162.1 27.8 %all-to-all-start.4 = ((bf16[8,64,768]{2,1,0:T(8,128)(2,1)}), bf16[8,64,768]{2,1,0:T(8,128)(2,1)S(1)}, u32[]{:S(2)}, u32[]{:S(2)}) async-start(bf16[8,64,768]{2,1,0:T(8,128)(2,1)} %add_x.1), calls=%async_computation.4 | async-start | bytes 1572864 | tf_op jit(solution)/shard_map/all_to_all | solution.py:283
  168.0 1.0 copy-start
  169.6 10.0 %collective-permute-start.9 = (bf16[64,768]{1,0:T(8,128)(2,1)S(1)}, bf16[64,768]{1,0:T(8,128)(2,1)S(1)}, u32[]{:S(2)}, u32[]{:S(2)}) collective-permute-start(bf16[64,768]{1,0:T(8,128)(2,1)S(1)} %get-tuple-element.31), channel_id=1, source_target_pairs={{0,16},{16,32},{32,48},{48,0},{1,17},{17,33},{33,49},{49,1},{2,18}... | collective-permute-start | bytes 294920 | tf_op jit(solution)/shard_map/ppermute | solution.py:422
  171.9 7.6 %collective-permute-start.10 = (bf16[64,768]{1,0:T(8,128)(2,1)S(1)}, bf16[64,768]{1,0:T(8,128)(2,1)S(1)}, u32[]{:S(2)}, u32[]{:S(2)}) collective-permute-start(bf16[64,768]{1,0:T(8,128)(2,1)S(1)} %get-tuple-element.32), channel_id=1, source_target_pairs={{0,32},{16,48},{32,0},{48,16},{1,33},{17,49},{33,1},{49,17},{2,34}... | collective-permute-start | bytes 294920 | tf_op jit(solution)/shard_map/ppermute | solution.py:422
  176.4 5.7 %collective-permute-start.11 = (bf16[64,768]{1,0:T(8,128)(2,1)S(1)}, bf16[64,768]{1,0:T(8,128)(2,1)S(1)}, u32[]{:S(2)}, u32[]{:S(2)}) collective-permute-start(bf16[64,768]{1,0:T(8,128)(2,1)S(1)} %get-tuple-element.33), channel_id=1, source_target_pairs={{0,48},{16,0},{32,16},{48,32},{1,49},{17,1},{33,17},{49,33},{2,50}... | collective-permute-start | bytes 294920 | tf_op jit(solution)/shard_map/ppermute | solution.py:422
Sparse Core Ops, SparseCore 0:
  11.7 100.8 all-gather.1
  122.7 44.5 reduce-scatter.1
